TPU v7x, 128 devices: a whole 4x4x4 slice. The times are simulated.
128 devices in a mesh: pb: 2 (over z_lo), row: 16 (over x, y), col: 4 (over z_hi, core).
Axes of the slice: x: 4, y: 4, z: 4 (z_hi: 2, z_lo: 2; z = z_hi * 2 + z_lo), core: 2. Of those that a mesh axis runs over, the one named last changes fastest.
Arguments:
- chol: bfloat16 [256, 1344, 1344], P('pb', 'row', 'col'), may hold values from -0.29882812 to 0.29882812
- amplitudes: bfloat16 [144, 1200], P(None, 'row'), may hold values from -0.59765625 to 0.59765625
Outputs:
- dressed: bfloat16 [256, 1344, 1344], P(('pb', 'row', 'col'))
- fock: float32 [1344, 1344], P('row', 'col')
All inputs are finite; a program needn't handle non-finite values.
Results may differ from a plain program's by a relative error of at most 0.02.
Values may be sent and summed in bfloat16 or wider, within the bound.
No kernel may reach another device: no remote copies, remote signals or barrier semaphores. Data moves between devices by JAX's collectives and lax.ppermute only.
A program may use at most 128 MiB of HBM per device.

v0:
```python
import functools

import jax
import jax.numpy as jnp
from jax import lax
from jax.sharding import Mesh
from jax.sharding import PartitionSpec as P

OCC = 144
OG = 9
VG = 75
SH = 84
NORB = 1344
ROW = ("row_0", "row_1")
ROW_COL = ("row_0", "row_1", "col")
PB_ROW_COL = ("pb", "row_0", "row_1", "col")


def copy_for_each(array, axis):
    copies = jnp.broadcast_to(array, (lax.axis_size(axis), *array.shape))
    return lax.all_to_all(copies, axis, split_axis=0, concat_axis=0, tiled=True)


def joined_along(pieces, dim):
    pieces = jnp.moveaxis(pieces, 0, dim)
    dims = pieces.shape
    return pieces.reshape(*dims[:dim], dims[dim] * dims[dim + 1], *dims[dim + 2 :])


def gathered_copies(array, axis, dim):
    pieces = copy_for_each(array, axis)
    return joined_along(pieces, dim)


def one_axis_at_a_time(array, axes):
    return functools.reduce(lax.psum, axes, array)


def over_copies(array, axis):
    everything = copy_for_each(array, axis)
    return jnp.sum(everything.astype(jnp.float32), axis=0)


def local(chol, amplitudes):
    q_local, row_width, col_width = chol.shape
    row_groups = row_width // SH
    col_groups = col_width // SH
    row_count = lax.axis_size(ROW)
    col_count = lax.axis_size("col")
    row_index = lax.axis_index(ROW)
    col_index = lax.axis_index("col")
    amp_table = gathered_copies(amplitudes, ROW, 1)
    layered = chol.reshape(q_local, row_groups, SH, col_width)
    vir_rows = layered[:, :, OG:, :].reshape(q_local, row_groups * VG, col_width)
    shift = lax.psum_scatter(
        jnp.einsum("ia,qac->iqc", amplitudes, vir_rows, preferred_element_type=jnp.float32).astype(
            jnp.bfloat16
        ),
        ROW,
        scatter_dimension=0,
        tiled=True,
    ).astype(jnp.float32)
    shift = jnp.transpose(shift.reshape(row_groups, OG, q_local, col_width), (2, 0, 1, 3))
    occ_new = (layered[:, :, :OG, :].astype(jnp.float32) - shift).astype(jnp.bfloat16)
    primed = jnp.concatenate([occ_new, layered[:, :, OG:, :]], axis=2).reshape(
        q_local, row_width, col_width
    )
    primed_cols = primed.reshape(q_local, row_width, col_groups, SH)
    local_occ = primed_cols[..., :OG].reshape(q_local, row_width, col_groups * OG)
    all_occ = lax.all_gather(local_occ, "col", axis=2, tiled=True)
    amp_cols = lax.dynamic_slice_in_dim(amp_table, col_index * col_groups * VG, col_groups * VG, 1)
    extra = jnp.einsum("qpi,ia->qpa", all_occ, amp_cols, preferred_element_type=jnp.float32)
    extra = extra.reshape(q_local, row_width, col_groups, VG)
    dressed_vir = (primed_cols[..., OG:].astype(jnp.float32) + extra).astype(jnp.bfloat16)
    dressed = jnp.concatenate([primed_cols[..., :OG], dressed_vir], axis=3).reshape(
        q_local, row_width, col_width
    )
    stacked = dressed.reshape(q_local, 1, row_width, col_width)
    arrived = lax.all_to_all(stacked, ROW_COL, split_axis=0, concat_axis=1, tiled=True)
    q_out = arrived.shape[0]
    arrived = arrived.reshape(q_out, row_count, col_count, row_width, col_width)
    whole_vectors = jnp.transpose(arrived, (0, 1, 3, 2, 4)).reshape(q_out, NORB, NORB)
    local_rows = dressed.reshape(q_local, row_groups, SH, col_width)[:, :, :OG, :]
    local_rows = local_rows.reshape(q_local, row_groups * OG, col_width)
    occ_rows = lax.all_gather(local_rows, ROW, axis=1, tiled=True)
    own_diag = all_occ.reshape(q_local, row_groups, SH, OCC)[:, :, :OG, :].reshape(
        q_local, row_groups * OG, OCC
    )
    own_diag = lax.dynamic_slice_in_dim(own_diag, row_index * row_groups * OG, row_groups * OG, 2)
    part_trace = jnp.trace(own_diag.astype(jnp.float32), axis1=1, axis2=2)
    weight = one_axis_at_a_time(part_trace, ROW)
    coulomb = jnp.einsum("q,qab->ab", weight, dressed.astype(jnp.float32))
    swapped = lax.dot_general(
        all_occ, occ_rows, (((0, 2), (0, 1)), ((), ())), preferred_element_type=jnp.float32
    )
    fock = over_copies((2.0 * coulomb - swapped).astype(jnp.bfloat16), "pb").astype(jnp.float32)
    return (whole_vectors, fock)


def solution(mesh):
    finer = Mesh(
        mesh.devices.reshape(mesh.shape["pb"], 4, 4, mesh.shape["col"]),
        ("pb", "row_0", "row_1", "col"),
    )
    placed = (P("pb", ROW, "col"), P(None, ROW))
    return jax.shard_map(
        local,
        mesh=finer,
        in_specs=placed,
        out_specs=(P(PB_ROW_COL, None, None), P(ROW, "col")),
        check_vma=False,
    )
```

profile of v0, /device:TPU:0, one launch (start us, length us, event | category | flops | bytes accessed | tf_op | source)
XLA Modules:
  0.0 449.3 jit_solution(14533646854765096088)
XLA Ops:
  7.2 0.0 copy-start.3
  7.2 0.0 reduce-scatter.4.cloned.1.call-start
  7.2 8.1 %copy.65 = bf16[128,84,336]{0,1,2:T(8,128)(2,1)} copy(bf16[128,84,336]{0,2,1:T(8,128)(2,1)} %param.2) | data formatting | bytes 14450688 | tf_op args[0]
  15.3 0.0 copy-done.3
  15.3 10.0 %convolution_convert_fusion = bf16[144,128,336]{1,0,2:T(8,128)(2,1)} fusion(bf16[144,75]{1,0:T(8,128)(2,1)S(1)} %copy-done.3, bf16[128,1,84,336]{0,2,3,1:T(8,128)(2,1)} %bitcast.62), kind=kOutput, calls=%fused_computation.8 | convolution fusion | flops 935165952 | bytes 19289184 | tf_op jit(solution)/shard_map/ia,qac->iqc/dot_general | solution.py:56
  25.3 13.5 %copy.46 = bf16[144,128,336]{1,2,0:T(8,128)(2,1)} copy(bf16[144,128,336]{1,0,2:T(8,128)(2,1)} %convolution_convert_fusion) | data formatting | bytes 24772608 | tf_op jit(solution)/shard_map/convert_element_type | solution.py:56
  38.8 0.0 reduce-scatter.4.cloned.1.call-update
  38.8 0.2 all-gather.4.cloned.1.call-start
  39.1 9.6 %slice.27 = bf16[128,1,75,336]{0,2,3,1:T(8,128)(2,1)} slice(bf16[128,1,84,336]{0,2,3,1:T(8,128)(2,1)} %bitcast.63), slice={[0:128], [0:1], [9:84], [0:336]} | slice | bytes 12902400 | tf_op jit(solution)/shard_map/slice | solution.py:54
  48.6 91.5 %reduce-scatter.4.cloned.1.call-done = bf16[9,128,336]{1,2,0:T(8,128)(2,1)} async-done(((bf16[144,128,336]{1,2,0:T(8,128)(2,1)}), bf16[9,128,336]{1,2,0:T(8,128)(2,1)}) %reduce-scatter.4.cloned.1.call-update) | async-done | bytes 774160
  140.2 1.9 fusion.8
  142.1 10.3 %pad_maximum_fusion = bf16[128,1,84,336]{0,2,3,1:T(8,128)(2,1)} fusion(bf16[128,1,75,336]{0,2,3,1:T(8,128)(2,1)} %slice.27, bf16[128,1,9,336]{0,2,3,1:T(8,128)(2,1)S(1)} %fusion.8), kind=kLoop, calls=%fused_computation.3 | loop fusion | flops 14450688 | bytes 14450688 | tf_op jit(solution)/shard_map/concatenate | solution.py:65
  152.4 2.1 slice.28
  154.5 0.0 all-gather.4.cloned.1.call-update
  154.5 0.9 broadcast_in_dim.15
  155.4 5.1 %all-to-all-start = ((bf16[16,144,75]{2,1,0:T(8,128)(2,1)}), bf16[16,144,75]{2,1,0:T(8,128)(2,1)S(1)}, u32[]{:S(2)}, u32[]{:S(2)}) async-start(bf16[16,144,75]{2,1,0:T(8,128)(2,1)} %broadcast_in_dim.15), calls=%async_computation | async-start | bytes 1179648 | tf_op jit(solution)/shard_map/all_to_all | solution.py:21
  160.5 0.3 all-gather.6.cloned.1.call-start
  160.8 10.2 %all-to-all-done = bf16[16,144,75]{2,1,0:T(8,128)(2,1)S(1)} async-done(((bf16[16,144,75]{2,1,0:T(8,128)(2,1)}), bf16[16,144,75]{2,1,0:T(8,128)(2,1)S(1)}, u32[]{:S(2)}, u32[]{:S(2)}) %all-to-all-start) | async-done | bytes 345632 | tf_op jit(solution)/shard_map/all_to_all | solution.py:21
  171.0 0.2 copy.48
  171.1 0.6 reshape.47
  171.7 15.8 %all-gather.4.cloned.1.call-done = bf16[128,84,144]{0,1,2:T(8,128)(2,1)} async-done(((bf16[128,84,36]{0,1,2:T(8,128)(2,1)}), bf16[128,84,144]{0,1,2:T(8,128)(2,1)}) %all-gather.4.cloned.1.call-update) | async-done | bytes 3096592 | tf_op jit(solution)/shard_map/all_gather | solution.py:70
  187.5 8.7 %fusion.5 = f32[128,84,300]{0,2,1:T(8,128)} fusion(bf16[128,84,144]{0,1,2:T(8,128)(2,1)} %all-gather.4.cloned.1.call-done, bf16[144,1200]{1,0:T(8,128)(2,1)S(1)} %reshape.47, s32[]{:T(128)S(6)} %select_n.11), kind=kOutput, calls=%fused_computation.10 | convolution fusion | flops 928972800 | bytes 16109572 | tf_op jit(solution)/shard_map/qpi,ia->qpa/dot_general | solution.py:72
  196.2 13.7 %copy.50 = f32[128,84,300]{0,1,2:T(8,128)} copy(f32[128,84,300]{0,2,1:T(8,128)} %fusion.5) | data formatting | bytes 25804800 | tf_op jit(solution)/shard_map/qpi,ia->qpa/dot_general | solution.py:72
  209.9 10.7 %add_convert_fusion = bf16[128,84,4,75]{0,1,3,2:T(8,128)(2,1)} fusion(f32[128,84,4,75]{0,1,3,2:T(8,128)} %bitcast.68, bf16[128,84,4,84]{0,1,3,2:T(8,128)(2,1)} %bitcast.70), kind=kLoop, calls=%fused_computation | loop fusion | flops 9676800 | bytes 25804800 | tf_op jit(solution)/shard_map/convert_element_type | solution.py:74
  220.6 0.0 copy-done.2
  220.6 3.6 pad_maximum_fusion.1
  224.2 0.0 copy-start
  224.2 3.1 copy-done
  227.3 0.2 slice.31
  227.6 1.1 copy.53
  228.7 0.0 all-gather.6.cloned.1.call-update
  228.7 13.1 %copy.51 = bf16[128,1,84,336]{3,2,1,0:T(8,128)(2,1)} copy(bf16[128,1,84,336]{0,2,3,1:T(8,128)(2,1)} %bitcast.66) | data formatting | bytes 14450688 | tf_op jit(solution)/shard_map/reshape;reshape | solution.py:78
  241.8 8.2 %all-to-all-start.1 = ((bf16[128,1,84,336]{3,2,1,0:T(8,128)(2,1)}), bf16[128,1,84,336]{3,2,1,0:T(8,128)(2,1)}, u32[]{:S(2)}, u32[]{:S(2)}) async-start(bf16[128,1,84,336]{3,2,1,0:T(8,128)(2,1)} %copy.51), calls=%async_computation.1 | async-start | bytes 17301504 | tf_op jit(solution)/shard_map/all_to_all | solution.py:79
  250.0 0.0 copy-done.1
  250.0 0.1 slice.30
  250.1 0.1 fusion.20
  250.2 133.2 %psum.14 = f32[128]{0:T(128)S(1)} all-reduce(f32[128]{0:T(128)S(1)} %fusion.20), channel_id=1, replica_groups=mesh['pb'=2,'row_0'=4,'row_1'=4,'col'=4] {'row_0'}, use_global_device_ids=true, to_apply=%region_2.3 | all-reduce | flops 128 | bytes 1024 | tf_op jit(solution)/shard_map/psum | solution.py:36
  383.4 16.4 %psum.15 = bf16[128]{0:T(256)(128)(2,1)S(1)} all-reduce(f32[128]{0:T(128)S(1)} %psum.14), channel_id=1, replica_groups=mesh['pb'=2,'row_0'=4,'row_1'=4,'col'=4] {'row_1'}, use_global_device_ids=true, to_apply=%region_3.4 | all-reduce | flops 128 | bytes 768 | tf_op jit(solution)/shard_map/psum | solution.py:36
  399.8 5.8 %fusion.2 = f32[1,84,336]{2,0,1:T(1,128)S(1)} fusion(bf16[128,84,336]{0,1,2:T(8,128)(2,1)} %bitcast.67, bf16[128]{0:T(256)(128)(2,1)S(1)} %psum.15), kind=kOutput, calls=%fused_computation.6 | convolution fusion | flops 7225344 | bytes 7338496 | tf_op jit(solution)/shard_map/q,qab->ab/dot_general | solution.py:92
  405.7 1.2 all-gather.6.cloned.1.call-done
  406.8 8.3 %fusion.15 = bf16[84,336]{1,0:T(8,128)(2,1)S(1)} fusion(bf16[128,84,144]{0,1,2:T(8,128)(2,1)S(1)} %copy-done.1, bf16[128,1,144,336]{0,3,1,2:T(8,128)(2,1)} %all-gather.6.cloned.1.call-done, f32[1,84,336]{2,0,1:T(1,128)S(1)} %fusion.2), kind=kOutput, calls=%fused_computation.17 | convolution fusion | flops 1040534208 | bytes 15652224 | tf_op jit(solution)/shard_map/dot_general | solution.py:93
  415.1 0.0 all-to-all-done.1
  415.1 0.7 broadcast_in_dim.18
  415.8 3.4 all-to-all-start.2
  419.2 8.4 %copy.52 = bf16[2,16,84,4,336]{4,3,2,1,0:T(4,128)(2,1)} copy(bf16[2,16,84,4,336]{4,2,0,3,1:T(8,128)(2,1)} %bitcast.14) | data formatting | bytes 14450688 | tf_op jit(solution)/shard_map/transpose | solution.py:82
  427.5 14.5 %reshape.50 = bf16[2,1344,1344]{2,1,0:T(8,128)(2,1)} reshape(bf16[2,16,84,4,336]{4,3,2,1,0:T(4,128)(2,1)} %copy.52) | data formatting | bytes 14450688 | tf_op jit(solution)/shard_map/reshape | solution.py:82
  442.1 0.0 all-to-all-done.2
  442.1 0.7 convert_reduce_fusion
  (3 shorter events, 0.0 us)
Async XLA Ops:
  7.2 8.1 %copy-start.3 = (bf16[144,75]{1,0:T(8,128)(2,1)S(1)}, bf16[144,75]{1,0:T(8,128)(2,1)}, u32[]{:S(2)}) copy-start(bf16[144,75]{1,0:T(8,128)(2,1)} %param.3) | copy-start | bytes 64804
  7.2 133.0 %reduce-scatter.4.cloned.1.call-start = ((), (), s32[]{:S(2)}) async-start(), calls=%async_computation.6 | async-start | bytes 13160448
  38.8 148.6 %all-gather.4.cloned.1.call-start = ((), (), s32[]{:S(2)}) async-start(), calls=%async_computation.4 | async-start | bytes 4055040 | tf_op jit(solution)/shard_map/all_gather | solution.py:70
  155.4 15.6 %all-to-all-start = ((bf16[16,144,75]{2,1,0:T(8,128)(2,1)}), bf16[16,144,75]{2,1,0:T(8,128)(2,1)S(1)}, u32[]{:S(2)}, u32[]{:S(2)}) async-start(bf16[16,144,75]{2,1,0:T(8,128)(2,1)} %broadcast_in_dim.15), calls=%async_computation | async-start | bytes 1179648 | tf_op jit(solution)/shard_map/all_to_all | solution.py:21
  160.5 246.3 %all-gather.6.cloned.1.call-start = ((), (), s32[]{:S(2)}) async-start(), calls=%async_computation.5 | async-start | bytes 13160448 | tf_op jit(solution)/shard_map/all_gather | solution.py:85
  209.9 10.7 %copy-start.2 = (bf16[128,84,4,9]{0,1,3,2:T(8,128)(2,1)S(1)}, bf16[128,84,4,9]{0,1,3,2:T(8,128)(2,1)}, u32[]{:S(2)}) copy-start(bf16[128,84,4,9]{0,1,3,2:T(8,128)(2,1)} %slice.28) | copy-start | bytes 2322436
  224.2 3.1 copy-start
  241.8 8.2 %copy-start.1 = (bf16[128,84,144]{0,1,2:T(8,128)(2,1)S(1)}, bf16[128,84,144]{0,1,2:T(8,128)(2,1)}, u32[]{:S(2)}) copy-start(bf16[128,84,144]{0,1,2:T(8,128)(2,1)} %all-gather.4.cloned.1.call-done) | copy-start | bytes 9289732
  241.8 173.3 %all-to-all-start.1 = ((bf16[128,1,84,336]{3,2,1,0:T(8,128)(2,1)}), bf16[128,1,84,336]{3,2,1,0:T(8,128)(2,1)}, u32[]{:S(2)}, u32[]{:S(2)}) async-start(bf16[128,1,84,336]{3,2,1,0:T(8,128)(2,1)} %copy.51), calls=%async_computation.1 | async-start | bytes 17301504 | tf_op jit(solution)/shard_map/all_to_all | solution.py:79
  415.8 26.3 %all-to-all-start.2 = ((bf16[2,84,336]{2,1,0:T(8,128)(2,1)}), bf16[2,84,336]{2,1,0:T(8,128)(2,1)S(1)}, u32[]{:S(2)}, u32[]{:S(2)}) async-start(bf16[2,84,336]{2,1,0:T(8,128)(2,1)} %broadcast_in_dim.18), calls=%async_computation.2 | async-start | bytes 270336 | tf_op jit(solution)/shard_map/all_to_all | solution.py:21
Sparse Core Ops, SparseCore 0:
  39.0 101.1 reduce-scatter.3
  154.6 32.8 all-gather.3
  228.9 177.9 all-gather.5
where the time goes:
time: 458 us; the launch traced here: 449 us
  blocking collectives  150 us (33%)
  waiting for transfers between devices  119 us (26%)
  local copies, waits for them, and re-layouts  89.8 us (20%)
  matrix products  32.8 us (7%)
  other arithmetic  27.3 us (6%)
  starting transfers between devices  17.2 us (4%)
  between operations  13.9 us (3%)
    psum x2, blocking collectives, one_axis_at_a_time(): return functools.reduce(lax.psum, axes, array)  150 us
    unnamed x4, waiting for transfers between devices  91.6 us
    all_gather x1, waiting for transfers between devices, local(): all_occ = lax.all_gather(local_occ, 'col', axis=2, tiled=True)  15.8 us
    reshape x1, local copies, waits for them, and re-layouts, local(): jnp.transpose(arrived, (0, 1, 3, 2, 4)).reshape(q_out, NORB, NORB)  14.5 us
    dot_general x1, local copies, waits for them, and re-layouts, local(): jnp.einsum('qpi,ia->qpa', all_occ, amp_cols, preferred_element_type=jnp.f...  13.7 us
    convert_element_type x1, local copies, waits for them, and re-layouts, local(): jnp.einsum('ia,qac->iqc', amplitudes, vir_rows, preferred_element_type=jn...  13.5 us
    another operation x1, local copies, waits for them, and re-layouts, local(): stacked = dressed.reshape(q_local, 1, row_width, col_width)  13.1 us
    unnamed x9, local copies, waits for them, and re-layouts  11.2 us
  transfers between devices with their start and end apart: 6, of which 4 were waited for; matrix products, arithmetic and copies ran while one was open for 14% of the time, Pallas kernels for 0%

commit v1 on v0

v1 whole, which is shorter than its diff:
```python
import jax
import jax.numpy as jnp
from jax import lax
from jax.sharding import Mesh
from jax.sharding import PartitionSpec as P

OG = 9
SH = 84
ROW = ("row_0", "row_1")
ALL = ("row_0", "row_1", "col_0", "col_1")


def gathered_copies(array, axis):
    copies = jnp.broadcast_to(array, (lax.axis_size(axis), *array.shape))
    return lax.all_to_all(copies, axis, split_axis=0, concat_axis=0, tiled=True)


def local(chol, amplitudes):
    q_local, row_width, col_width = chol.shape
    rows, cols = lax.axis_size(ROW), lax.axis_size(("col_0", "col_1"))
    q_own = q_local // (rows * cols)
    norb = rows * row_width
    groups = norb // SH
    pieces = lax.all_to_all(chol[:, None], ALL, split_axis=0, concat_axis=1, tiled=True)
    amp = gathered_copies(amplitudes, ROW)
    amp = jnp.transpose(amp, (1, 0, 2)).reshape(groups, OG, groups, SH - OG)
    amp = jnp.pad(amp, ((0, 0), (0, SH - OG), (0, 0), (OG, 0))).reshape(norb, norb)
    eye = jnp.eye(norb, dtype=jnp.bfloat16)
    pieces = pieces.reshape(q_own, rows, cols, row_width, col_width)
    whole = jnp.transpose(pieces, (0, 1, 3, 2, 4)).reshape(q_own, norb, norb)
    primed = jnp.einsum("pr,qrs->qps", eye - amp, whole, preferred_element_type=jnp.float32)
    primed = primed.astype(jnp.bfloat16)
    dressed = jnp.einsum("qpr,rs->qps", primed, eye + amp, preferred_element_type=jnp.float32)
    dressed = dressed.astype(jnp.bfloat16)
    occupied = jnp.arange(norb) % SH < OG
    diagonal = jnp.diagonal(dressed, axis1=1, axis2=2).astype(jnp.float32)
    weight = jnp.sum(jnp.where(occupied, diagonal, 0.0), axis=1)
    occ_cols = jnp.where(occupied, dressed, jnp.zeros_like(dressed))
    swapped = jnp.einsum("qpi,qir->pr", occ_cols, dressed, preferred_element_type=jnp.float32)
    fock = 2.0 * jnp.einsum("q,qpr->pr", weight, dressed.astype(jnp.float32)) - swapped
    fock = fock.astype(jnp.bfloat16).reshape(rows, row_width, cols // 2, 2, col_width)
    fock = jnp.transpose(fock, (3, 0, 2, 1, 4))
    fock = lax.all_to_all(fock, "col_1", split_axis=0, concat_axis=0, tiled=True)
    fock = jnp.sum(fock.astype(jnp.float32), axis=0).astype(jnp.bfloat16)
    fock = fock.reshape(rows * cols // 2, row_width, col_width)
    fock = lax.all_to_all(fock, (*ROW, "col_0"), split_axis=0, concat_axis=0, tiled=True)
    fock = jnp.sum(fock.astype(jnp.float32), axis=0).astype(jnp.bfloat16)
    other = lax.ppermute(fock, "pb", ((0, 1), (1, 0)))
    return dressed, fock.astype(jnp.float32) + other.astype(jnp.float32)


def solution(mesh):
    finer = Mesh(
        mesh.devices.reshape(mesh.shape["pb"], 4, 4, mesh.shape["col"] // 2, 2),
        ("pb", *ALL),
    )
    placed = (P("pb", ROW, ("col_0", "col_1")), P(None, ROW))
    return jax.shard_map(
        local,
        mesh=finer,
        in_specs=placed,
        out_specs=(P(("pb", *ALL), None, None), P(ROW, ("col_0", "col_1"))),
        check_vma=False,
    )
```

time: 458 us -> 364 us (0.79)
  blocking collectives: 150 us -> 60 us
  waiting for transfers between devices: 119 us -> 83.8 us
  local copies, waits for them, and re-layouts: 89.8 us -> 120 us
  matrix products: 32.8 us -> 55.6 us
  between operations: 13.9 us -> 1.17 us
  other arithmetic: 27.3 us -> 16.5 us
    psum x2 -> x0, blocking collectives: 150 us -> none  [one_axis_at_a_time(): return functools.reduce(lax.psum, axes, array)]
    unnamed x4 -> x0, waiting for transfers between devices: 91.6 us -> none
    all_to_all x3 -> x2, waiting for transfers between devices: 10.2 us -> 80.5 us  [the longest x1 80 us: local(): lax.all_to_all(chol[:, None], ALL, split_axis=0, concat_axis=1, tiled=True)]
    all_to_all x0 -> x2, blocking collectives: none -> 60 us  [the longest x1 47.3 us: local(): lax.all_to_all(fock, (*ROW, 'col_0'), split_axis=0, concat_axis=0, tiled=...]
    reshape x2 -> x5, local copies, waits for them, and re-layouts: 15.1 us -> 49.4 us  [the longest x2 16.5 us: local(): fock.astype(jnp.bfloat16).reshape(rows, row_width, cols // 2, 2, col_width)]
    dot_general x4 -> x3, matrix products: 32.8 us -> 55.6 us  [the longest x1 31.6 us: local(): jnp.einsum('qpr,rs->qps', primed, eye + amp, preferred_element_type=jnp.f...]
    convert_element_type x1, local copies, waits for them, and re-layouts: 13.5 us -> 31.8 us  [local(): dressed = dressed.astype(jnp.bfloat16)]
    all_gather x2 -> x0, waiting for transfers between devices: 16.9 us -> none  [the longest x1 15.8 us: local(): all_occ = lax.all_gather(local_occ, 'col', axis=2, tiled=True)]
  transfers between devices with their start and end apart: 6 -> 3, of which waited for: 4 -> 3; matrix products, arithmetic and copies ran while one was open for 14% -> 11% of each run, Pallas kernels for 0% -> 0%
where the time goes in v1:
time: 364 us; the launch traced here: 357 us
  local copies, waits for them, and re-layouts  120 us (33%)
  waiting for transfers between devices  83.8 us (23%)
  blocking collectives  60 us (16%)
  matrix products  55.6 us (15%)
  starting transfers between devices  19.4 us (5%)
  other arithmetic  16.5 us (5%)
    all_to_all x1, waiting for transfers between devices, local(): lax.all_to_all(chol[:, None], ALL, split_axis=0, concat_axis=1, tiled=True)  80 us
    all_to_all x1, blocking collectives, local(): lax.all_to_all(fock, (*ROW, 'col_0'), split_axis=0, concat_axis=0, tiled=...  47.3 us
    convert_element_type x1, local copies, waits for them, and re-layouts, local(): dressed = dressed.astype(jnp.bfloat16)  31.8 us
    dot_general x1, matrix products, local(): jnp.einsum('qpr,rs->qps', primed, eye + amp, preferred_element_type=jnp.f...  31.6 us
    reshape x2, local copies, waits for them, and re-layouts, local(): fock.astype(jnp.bfloat16).reshape(rows, row_width, cols // 2, 2, col_width)  16.5 us
    gather x1, local copies, waits for them, and re-layouts, local(): diagonal = jnp.diagonal(dressed, axis1=1, axis2=2).astype(jnp.float32)  15.2 us
    reshape x1, local copies, waits for them, and re-layouts, local(): whole = jnp.transpose(pieces, (0, 1, 3, 2, 4)).reshape(q_own, norb, norb)  14.5 us
    dot_general x1, matrix products, local(): jnp.einsum('qpi,qir->pr', occ_cols, dressed, preferred_element_type=jnp.f...  13.6 us
  transfers between devices with their start and end apart: 3, of which 3 were waited for; matrix products, arithmetic and copies ran while one was open for 11% of the time, Pallas kernels for 0%

profile of v1, /device:TPU:0, one launch (start us, length us, event | category | flops | bytes accessed | tf_op | source)
XLA Modules:
  0.0 356.9 jit_solution(9368244337582809766)
XLA Ops:
  0.6 1.7 broadcast_in_dim.25
  2.3 7.1 %all-to-all-start = ((bf16[16,144,75]{2,1,0:T(8,128)(2,1)}), bf16[16,144,75]{2,1,0:T(8,128)(2,1)S(1)}, u32[]{:S(2)}, u32[]{:S(2)}) async-start(bf16[16,144,75]{2,1,0:T(8,128)(2,1)} %broadcast_in_dim.25), calls=%async_computation | async-start | bytes 1179648 | tf_op jit(solution)/shard_map/all_to_all | solution.py:15
  9.4 11.7 %copy.16 = bf16[128,84,336]{2,1,0:T(8,128)(2,1)} copy(bf16[128,84,336]{0,2,1:T(8,128)(2,1)} %param.2) | data formatting | bytes 14450688 | tf_op args[0]
  21.2 0.5 all-to-all-done
  21.6 11.2 %all-to-all-start.1 = ((bf16[128,1,84,336]{3,2,1,0:T(8,128)(2,1)}), bf16[128,1,84,336]{3,2,1,0:T(8,128)(2,1)}, u32[]{:S(2)}, u32[]{:S(2)}) async-start(bf16[128,1,84,336]{3,2,1,0:T(8,128)(2,1)} %bitcast.57), calls=%async_computation.1 | async-start | bytes 17301504 | tf_op jit(solution)/shard_map/all_to_all | solution.py:24
  32.9 0.2 copy.15
  33.1 5.8 %fusion.26 = (bf16[16,84,16,84]{3,2,1,0:T(8,128)(2,1)}, bf16[16,84,16,84]{3,2,1,0:T(8,128)(2,1)}) fusion(bf16[16,9,16,75]{3,2,1,0:T(8,128)(2,1)S(1)} %bitcast.63, s32[16,84]{1,0:T(8,128)S(1)} %multiply_add_fusion), kind=kLoop, calls=%fused_computation.33 | loop fusion | flops 10838016 | bytes 7576320 | tf_op jit(solution)/shard_map/jit(_pad)/pad | solution.py:27
  38.9 10.1 %reshape.45 = bf16[1344,1344]{1,0:T(8,128)(2,1)} reshape(bf16[16,84,16,84]{3,2,1,0:T(8,128)(2,1)} %get-tuple-element.2) | data formatting | bytes 7225344 | tf_op jit(solution)/shard_map/reshape | solution.py:27
  49.0 10.1 %reshape.54 = bf16[1344,1344,1]{1,0,2:T(8,128)(2,1)} reshape(bf16[16,84,16,84]{3,2,1,0:T(8,128)(2,1)} %get-tuple-element.3) | data formatting | bytes 7225344 | tf_op jit(solution)/shard_map/sub | solution.py:31
  59.1 80.0 %all-to-all-done.1 = bf16[128,1,84,336]{3,2,1,0:T(8,128)(2,1)} async-done(((bf16[128,1,84,336]{3,2,1,0:T(8,128)(2,1)}), bf16[128,1,84,336]{3,2,1,0:T(8,128)(2,1)}, u32[]{:S(2)}, u32[]{:S(2)}) %all-to-all-start.1) | async-done | bytes 7225376 | tf_op jit(solution)/shard_map/all_to_all | solution.py:24
  139.1 8.3 %copy.29 = bf16[2,16,4,84,336]{4,2,3,1,0:T(4,128)(2,1)} copy(bf16[2,16,4,84,336]{4,3,0,2,1:T(8,128)(2,1)} %bitcast.5) | data formatting | bytes 14450688 | tf_op jit(solution)/shard_map/reshape | solution.py:29
  147.5 14.5 %reshape.44 = bf16[2,1344,1344]{2,1,0:T(8,128)(2,1)} reshape(bf16[2,16,84,4,336]{4,3,2,1,0:T(4,128)(2,1)} %bitcast.58) | data formatting | bytes 14450688 | tf_op jit(solution)/shard_map/reshape | solution.py:30
  162.0 31.6 %convolution_convert_fusion = bf16[2,1344,1344]{2,1,0:T(8,128)(2,1)} fusion(bf16[1344,1344]{1,0:T(8,128)(2,1)} %reshape.45, bf16[1344,1344,1]{1,0,2:T(8,128)(2,1)} %reshape.54, bf16[2,1344,1344]{2,1,0:T(8,128)(2,1)} %reshape.44), kind=kOutput, calls=%fused_computation.4 | convolution fusion | flops 19439788032 | bytes 21676032 | tf_op jit(solution)/shard_map/qpr,rs->qps/dot_general | solution.py:33
  193.6 31.8 %copy.18 = bf16[2,1344,1344]{2,0,1:T(2,128)(2,1)} copy(bf16[2,1344,1344]{2,1,0:T(8,128)(2,1)} %convolution_convert_fusion) | data formatting | bytes 14450688 | tf_op jit(solution)/shard_map/convert_element_type | solution.py:34
  225.4 0.0 slice-start
  225.4 15.2 %gather_fusion = bf16[1344,2]{0,1:T(2,128)(2,1)S(1)} fusion(bf16[2,1344,1344]{2,0,1:T(2,128)(2,1)} %copy.18, s32[1344]{0:T(1024)S(1)} %or_reduce_fusion), kind=kCustom, calls=%fused_computation | custom fusion | bytes 21504 | tf_op jit(solution)/shard_map/jit(diagonal)/gather | solution.py:36
  240.6 0.1 select_reduce_fusion
  240.8 0.0 slice-start.1
  240.8 10.4 %fusion.23 = f32[1,1344,1344]{2,0,1:T(1,128)S(1)} fusion(bf16[2,1344,1344]{2,0,1:T(2,128)(2,1)} %copy.18, bf16[2]{0:T(256)(128)(2,1)S(1)} %select_reduce_fusion), kind=kOutput, calls=%fused_computation.30 | convolution fusion | flops 7225344 | bytes 14450692 | tf_op jit(solution)/shard_map/q,qpr->pr/dot_general | solution.py:40
  251.1 0.0 slice-done
  251.1 0.0 slice-done.1
  251.1 13.6 %fusion.11 = bf16[1344,1344]{1,0:T(8,128)(2,1)} fusion(bf16[2,1344,1344]{2,1,0:T(8,128)(2,1)S(1)} %bitcast.62, pred[1344]{0:T(1024)(128)(4,1)S(1)} %fusion.19, f32[1,1344,1344]{2,0,1:T(1,128)S(1)} %fusion.23), kind=kOutput, calls=%fused_computation.14 | convolution fusion | flops 9719894016 | bytes 18064704 | tf_op jit(solution)/shard_map/qpi,qir->pr/dot_general | solution.py:39
  264.8 11.2 %reshape.46 = bf16[16,84,2,2,336]{4,3,2,1,0:T(2,128)(2,1)} reshape(bf16[1344,1344]{1,0:T(8,128)(2,1)} %fusion.11) | data formatting | bytes 7225344 | tf_op jit(solution)/shard_map/reshape | solution.py:41
  276.0 5.4 %copy.30 = bf16[16,84,2,2,336]{4,2,1,0,3:T(2,128)(2,1)S(1)} copy(bf16[16,84,2,2,336]{4,3,2,1,0:T(2,128)(2,1)} %reshape.46) | data formatting | bytes 7225344 | tf_op jit(solution)/shard_map/reshape | solution.py:41
  281.3 12.7 %all_to_all.30 = bf16[2,16,2,84,336]{4,2,3,1,0:T(2,128)(2,1)} all-to-all(bf16[2,16,2,84,336]{4,2,3,1,0:T(2,128)(2,1)S(1)} %bitcast.59), channel_id=1, replica_groups=mesh['pb'=2,'row_0'=4,'row_1'=4,'col_0'=2,'col_1'=2] {'col_1'}, dimensions={0} | all-to-all | bytes 7225344 | tf_op jit(solution)/shard_map/all_to_all | solution.py:43
  294.0 9.4 %reduce_sum.34 = bf16[16,2,84,336]{3,1,2,0:T(2,128)(2,1)S(1)} reduce(bf16[2,16,2,84,336]{4,2,3,1,0:T(2,128)(2,1)} %all_to_all.30, bf16[]{:T(256)} %constant.26.clone.1), dimensions={0}, to_apply=%region_1.2 | reduce | flops 903168 | bytes 5419010 | tf_op jit(solution)/shard_map/reduce_sum | solution.py:44
  303.4 0.3 copy.21
  303.7 47.3 %all_to_all.31 = bf16[32,84,336]{2,1,0:T(8,128)(2,1)S(1)} all-to-all(bf16[32,84,336]{2,1,0:T(8,128)(2,1)S(1)} %bitcast.60), channel_id=1, replica_groups=mesh['pb'=2,'row_0'=4,'row_1'=4,'col_0'=2,'col_1'=2] {'row_0','row_1','c..., dimensions={0} | all-to-all | bytes 3612672 | tf_op jit(solution)/shard_map/all_to_all | solution.py:46
  351.0 0.4 reduce_sum.35
  351.4 1.1 collective-permute-start
  352.5 3.3 collective-permute-done
  355.8 0.7 convert_add_fusion
  (4 shorter events, 0.1 us)
Async XLA Ops:
  2.3 19.3 %all-to-all-start = ((bf16[16,144,75]{2,1,0:T(8,128)(2,1)}), bf16[16,144,75]{2,1,0:T(8,128)(2,1)S(1)}, u32[]{:S(2)}, u32[]{:S(2)}) async-start(bf16[16,144,75]{2,1,0:T(8,128)(2,1)} %broadcast_in_dim.25), calls=%async_computation | async-start | bytes 1179648 | tf_op jit(solution)/shard_map/all_to_all | solution.py:15
  21.6 117.5 %all-to-all-start.1 = ((bf16[128,1,84,336]{3,2,1,0:T(8,128)(2,1)}), bf16[128,1,84,336]{3,2,1,0:T(8,128)(2,1)}, u32[]{:S(2)}, u32[]{:S(2)}) async-start(bf16[128,1,84,336]{3,2,1,0:T(8,128)(2,1)} %bitcast.57), calls=%async_computation.1 | async-start | bytes 17301504 | tf_op jit(solution)/shard_map/all_to_all | solution.py:24
  225.4 25.7 %slice-start = ((s8[7569408]{0:T(1024)(128)(4,1)}), s8[3375104]{0:T(1024)(128)(4,1)S(1)}, s32[]{:S(2)}) async-start(s8[7569408]{0:T(1024)(128)(4,1)} %bitcast.61), calls=%async_computation.4 | async-start | bytes 6750208
  240.8 10.4 %slice-start.1 = ((s8[7569408]{0:T(1024)(128)(4,1)}), s8[4194304]{0:T(1024)(128)(4,1)S(1)}, s32[]{:S(2)}) async-start(s8[7569408]{0:T(1024)(128)(4,1)} %bitcast.61), calls=%async_computation.5 | async-start | bytes 8388608
  351.4 4.4 %collective-permute-start = (bf16[84,336]{1,0:T(8,128)(2,1)S(1)}, bf16[84,336]{1,0:T(8,128)(2,1)S(1)}, u32[]{:S(2)}, u32[]{:S(2)}) collective-permute-start(bf16[84,336]{1,0:T(8,128)(2,1)S(1)} %reduce_sum.35), channel_id=1, source_target_pairs={{0,64},{64,0},{1,65},{65,1},{2,66},{66,2},{3,67},{67,3},{4,68},{68... | collective-permute-start | bytes 169352 | tf_op jit(solution)/shard_map/ppermute | solution.py:48

commit v2 on v1

v2 whole, which is shorter than its diff:
```python
import functools
import jax
import jax.numpy as jnp
from jax import lax
from jax.experimental import pallas as pl
from jax.experimental.pallas import tpu as pltpu
from jax.sharding import Mesh
from jax.sharding import PartitionSpec as P

OG, SH = 9, 84
RP, CP, WIN = 96, 384, 16


def dress(own, last, pieces, win, cols, sel, *rest):
    if last:
        before, unused, whole, fock, x, occ, stage, sem = rest
    else:
        whole, fock, x, occ, stage, sem = rest
    rows = x.shape[0] // RP
    blocks = x.shape[1] // CP
    width = pieces.shape[-1]
    per = rows // blocks
    x[...] = jnp.zeros_like(x)

    def place(r, carry):
        for c in range(blocks):
            x[pl.ds(pl.multiple_of(r * RP, RP), SH), c * CP : c * CP + width] = pieces[r * blocks + c, 0]
        return carry

    lax.fori_loop(0, rows, place, 0)
    for c in range(blocks):
        lanes = slice(c * CP, (c + 1) * CP)
        shift = jnp.dot(win[...], x[:, lanes], preferred_element_type=jnp.float32)
        for r in range(rows):
            at = slice(r * RP, r * RP + WIN)
            fixed = x[at, lanes].astype(jnp.float32) - shift[r * WIN : (r + 1) * WIN]
            x[at, lanes] = fixed.astype(jnp.bfloat16)
    deep = per * RP
    tall = per * SH

    def columns(m, carry):
        at = pl.ds(pl.multiple_of(m * deep, deep), deep)
        old = x[at, :]
        g = jnp.dot(old, sel[...], preferred_element_type=jnp.float32).astype(jnp.bfloat16)
        occ[at, :] = g
        extra = jnp.dot(g, cols[...], preferred_element_type=jnp.float32)
        new = (old.astype(jnp.float32) + extra).astype(jnp.bfloat16)
        x[at, :] = new
        for r in range(per):
            for c in range(blocks):
                block = new[r * RP : r * RP + SH, c * CP : c * CP + width]
                stage[m, r * SH : (r + 1) * SH, c * width : (c + 1) * width] = block
        pltpu.make_async_copy(
            stage.at[m], whole.at[own, pl.ds(pl.multiple_of(m * tall, tall), tall)], sem.at[m]
        ).start()
        return carry

    lax.fori_loop(0, blocks, columns, 0)
    inner = jnp.concatenate([occ[r * RP : r * RP + WIN, :] for r in range(rows)], axis=0)
    here = lax.broadcasted_iota(jnp.int32, inner.shape, 0)
    there = lax.broadcasted_iota(jnp.int32, inner.shape, 1)
    weight = 2.0 * jnp.sum(jnp.where(here == there, inner.astype(jnp.float32), 0.0))
    occ_rows = jnp.concatenate([x[r * RP : r * RP + WIN, :] for r in range(rows)], axis=0)

    def total(m, carry):
        at = pl.ds(pl.multiple_of(m * deep, deep), deep)
        swapped = jnp.dot(occ[at, :], occ_rows, preferred_element_type=jnp.float32)
        part = weight * x[at, :].astype(jnp.float32) - swapped
        if last:
            part = (part + before[at, :]).astype(jnp.bfloat16)
            for r in range(per):
                for c in range(blocks):
                    block = part[r * RP : r * RP + SH, c * CP : c * CP + width]
                    fock[c % 2, (m * per + r) * (blocks // 2) + c // 2] = block
        else:
            fock[at, :] = part
        return carry

    lax.fori_loop(0, blocks, total, 0)
    for m in range(blocks):
        pltpu.make_async_copy(
            stage.at[m], whole.at[own, m * tall : (m + 1) * tall], sem.at[m]
        ).wait()


def dress_call(own, pieces, win, cols, sel, before=None, whole=None, q_own=2):
    last = before is not None
    rows = win.shape[0] // WIN
    blocks = pieces.shape[0] // rows
    norb = rows * SH
    width = pieces.shape[-1]
    vmem, hbm = pl.BlockSpec(memory_space=pltpu.VMEM), pl.BlockSpec(memory_space=pl.ANY)
    wide = rows * RP
    if last:
        fock = jax.ShapeDtypeStruct((2, rows * blocks // 2, SH, width), jnp.bfloat16)
    else:
        fock = jax.ShapeDtypeStruct((wide, blocks * CP), jnp.float32)
    args = (pieces, win, cols, sel) + ((before, whole) if last else ())
    return pl.pallas_call(
        functools.partial(dress, own, last),
        out_shape=(jax.ShapeDtypeStruct((q_own, norb, norb), jnp.bfloat16), fock),
        in_specs=[vmem] * 4 + ([vmem, hbm] if last else []),
        out_specs=(hbm, vmem),
        input_output_aliases={5: 0} if last else {},
        scratch_shapes=[
            pltpu.VMEM((wide, blocks * CP), jnp.bfloat16),
            pltpu.VMEM((wide, rows * WIN), jnp.bfloat16),
            pltpu.VMEM((blocks, rows // blocks * SH, norb), jnp.bfloat16),
            pltpu.SemaphoreType.DMA((blocks,)),
        ],
        compiler_params=pltpu.CompilerParams(vmem_limit_bytes=60 * 2**20),
        name="dress_last" if last else "dress_first",
    )(*args)


def tables(amp, blocks):
    groups = amp.shape[0]
    cut = amp.reshape(groups, groups, OG, SH - OG)
    cut = jnp.pad(cut, ((0, 0), (0, 0), (0, WIN - OG), (OG, 0))).reshape(groups, groups * WIN, SH)
    win = jnp.pad(cut, ((0, 0), (0, 0), (0, RP - SH)))
    win = jnp.transpose(win, (1, 0, 2)).reshape(groups * WIN, groups * RP)
    per = groups // blocks
    cols = jnp.transpose(cut, (1, 0, 2)).reshape(groups * WIN, blocks, per * SH)
    cols = jnp.pad(cols, ((0, 0), (0, 0), (0, CP - per * SH))).reshape(groups * WIN, blocks * CP)
    at = lax.broadcasted_iota(jnp.int32, (blocks * CP, groups * WIN), 0)
    to = lax.broadcasted_iota(jnp.int32, (blocks * CP, groups * WIN), 1)
    inside = at % CP
    group = at // CP * per + inside // SH
    hit = (inside < per * SH) & (to // WIN == group) & (to % WIN == inside % SH) & (inside % SH < OG)
    return win, cols, hit.astype(jnp.bfloat16)


ROW = ("row_0", "row_1")
COL = ("col_0", "col_1")
ALL = (*ROW, *COL)


def swap(array, axis):
    return lax.all_to_all(array, axis, split_axis=0, concat_axis=0, tiled=True)


def local(chol, amplitudes):
    q_local, row_width, col_width = chol.shape
    devices = lax.axis_size(ALL)
    cols = lax.axis_size(COL)
    q_own = q_local // devices
    sent = chol.reshape(devices, q_own, 1, row_width, col_width)
    first = swap(sent[:, 0], ALL)
    amp = swap(jnp.broadcast_to(amplitudes, (lax.axis_size(ROW), *amplitudes.shape)), ROW)
    win, into, sel = tables(amp, cols)
    second = swap(sent[:, 1], ALL)
    whole, part = dress_call(0, first, win, into, sel)
    whole, fock = dress_call(1, second, win, into, sel, part, whole)
    fock = swap(fock, "col_1")
    fock = (fock[0].astype(jnp.float32) + fock[1].astype(jnp.float32)).astype(jnp.bfloat16)
    fock = swap(fock, (*ROW, "col_0"))
    fock = jnp.sum(fock.astype(jnp.float32), axis=0).astype(jnp.bfloat16)
    other = lax.ppermute(fock, "pb", ((0, 1), (1, 0)))
    return whole, fock.astype(jnp.float32) + other.astype(jnp.float32)


def solution(mesh):
    finer = Mesh(
        mesh.devices.reshape(mesh.shape["pb"], 4, 4, mesh.shape["col"] // 2, 2),
        ("pb", *ALL),
    )
    placed = (P("pb", ROW, COL), P(None, ROW))
    return jax.shard_map(
        local,
        mesh=finer,
        in_specs=placed,
        out_specs=(P(("pb", *ALL), None, None), P(ROW, COL)),
        check_vma=False,
    )
```

time: 364 us -> 229 us (0.63); the launches traced: 357 us -> 228 us
  local copies, waits for them, and re-layouts: 120 us -> 30.5 us
  matrix products: 55.6 us -> 0 us
  waiting for transfers between devices: 83.8 us -> 28.4 us
  blocking collectives: 60 us -> 113 us
  Pallas kernels: 0 us -> 35.3 us
  other arithmetic: 16.5 us -> 5.06 us
  starting transfers between devices: 19.4 us -> 14.5 us
    dot_general x3 -> x0, matrix products: 55.6 us -> none  [the longest x1 31.6 us: local(): jnp.einsum('qpr,rs->qps', primed, eye + amp, preferred_element_type=jnp.f...]
    all_to_all x2, waiting for transfers between devices: 80.5 us -> 25.1 us  [swap(): return lax.all_to_all(array, axis, split_axis=0, concat_axis=0, tiled=True)]
    all_to_all x2 -> x3, blocking collectives: 60 us -> 113 us  [swap(): return lax.all_to_all(array, axis, split_axis=0, concat_axis=0, tiled=True)]
    reshape x5 -> x4, local copies, waits for them, and re-layouts: 49.4 us -> 4.63 us  [the longest x2 2.26 us: tables(): cols = jnp.transpose(cut, (1, 0, 2)).reshape(groups * WIN, blocks, per * SH)]
    pallas_call x0 -> x2, Pallas kernels: none -> 35.3 us  [dress_call(): pl.pallas_call(functools.partial(dress, own, last), out_shape=(jax.ShapeD...]
    convert_element_type x1, local copies, waits for them, and re-layouts: 31.8 us -> 0.73 us  [local(): (fock[0].astype(jnp.float32) + fock[1].astype(jnp.float32)).astype(jnp.bf...]
    gather x1 -> x0, local copies, waits for them, and re-layouts: 15.2 us -> none  [local(): diagonal = jnp.diagonal(dressed, axis1=1, axis2=2).astype(jnp.float32)]
    sub x1 -> x0, local copies, waits for them, and re-layouts: 10.1 us -> none  [local(): eye - amp]
  transfers between devices with their start and end apart: 3 -> 3, of which waited for: 3 -> 2; matrix products, arithmetic and copies ran while one was open for 11% -> 13% of each run, Pallas kernels for 0% -> 7%
where the time goes in v2:
time: 229 us; the launch traced here: 228 us
  blocking collectives  113 us (49%)
  Pallas kernels  35.3 us (15%)
  local copies, waits for them, and re-layouts  30.5 us (13%)
  waiting for transfers between devices  28.4 us (12%)
  starting transfers between devices  14.5 us (6%)
  other arithmetic  5.06 us (2%)
    all_to_all x3, blocking collectives, swap(): return lax.all_to_all(array, axis, split_axis=0, concat_axis=0, tiled=True)  113 us
    pallas_call x2, Pallas kernels, dress_call(): pl.pallas_call(functools.partial(dress, own, last), out_shape=(jax.ShapeD...  35.3 us
    all_to_all x2, waiting for transfers between devices, swap(): return lax.all_to_all(array, axis, split_axis=0, concat_axis=0, tiled=True)  25.1 us
    all_to_all x2, starting transfers between devices, swap(): return lax.all_to_all(array, axis, split_axis=0, concat_axis=0, tiled=True)  13.4 us
    unnamed x1, local copies, waits for them, and re-layouts  11.7 us
    squeeze x1, local copies, waits for them, and re-layouts, local(): first = swap(sent[:, 0], ALL)  6.25 us
  transfers between devices with their start and end apart: 3, of which 2 were waited for; matrix products, arithmetic and copies ran while one was open for 13% of the time, Pallas kernels for 7%

profile of v2, /device:TPU:0, one launch (start us, length us, event | category | flops | bytes accessed | tf_op | source)
XLA Modules:
  0.0 228.0 jit_solution(4397897287537879137)
XLA Ops:
  0.6 1.8 broadcast_in_dim.3
  2.4 7.1 %all-to-all-start.1 = ((bf16[16,144,75]{2,1,0:T(8,128)(2,1)}), bf16[16,144,75]{2,1,0:T(8,128)(2,1)S(1)}, u32[]{:S(2)}, u32[]{:S(2)}) async-start(bf16[16,144,75]{2,1,0:T(8,128)(2,1)} %broadcast_in_dim.3), calls=%async_computation.1 | async-start | bytes 1179648 | tf_op jit(solution)/shard_map/all_to_all | solution.py:139
  9.5 11.7 %copy.33 = bf16[128,84,336]{2,1,0:T(8,128)(2,1)} copy(bf16[128,84,336]{0,2,1:T(8,128)(2,1)} %param.2) | data formatting | bytes 14450688 | tf_op args[0]
  21.3 6.2 %slice_bitcast_fusion = (bf16[64,1,84,336]{3,2,1,0:T(8,128)(2,1)}, bf16[64,1,84,336]{3,2,1,0:T(8,128)(2,1)}) fusion(bf16[64,2,1,84,336]{4,3,1,0,2:T(8,128)(2,1)} %bitcast.19), kind=kLoop, calls=%fused_computation | loop fusion | bytes 14450688 | tf_op jit(solution)/shard_map/squeeze | solution.py:148
  27.5 0.0 all-to-all-done.1
  27.5 66.4 %all_to_all.25.pieces = bf16[64,1,84,336]{3,2,1,0:T(8,128)(2,1)} all-to-all(bf16[64,1,84,336]{3,2,1,0:T(8,128)(2,1)} %get-tuple-element.10), channel_id=1, replica_groups=mesh['pb'=2,'row_0'=4,'row_1'=4,'col_0'=2,'col_1'=2] {'row_0','row_1','c..., dimensions={0} | all-to-all | bytes 7225344 | tf_op jit(solution)/shard_map/all_to_all | solution.py:139
  93.9 6.2 %all-to-all-start = ((bf16[64,1,84,336]{3,2,1,0:T(8,128)(2,1)}), bf16[64,1,84,336]{3,2,1,0:T(8,128)(2,1)}, u32[]{:S(2)}, u32[]{:S(2)}) async-start(bf16[64,1,84,336]{3,2,1,0:T(8,128)(2,1)} %get-tuple-element.11), calls=%async_computation | async-start | bytes 8650752 | tf_op jit(solution)/shard_map/all_to_all | solution.py:139
  100.2 3.4 %fusion.15.sel = bf16[1536,256]{1,0:T(8,128)(2,1)} fusion(s32[256]{0:T(256)S(1)} %get-tuple-element.19, s32[256]{0:T(256)S(1)} %get-tuple-element.22, s32[1536]{0:T(1024)S(1)} %get-tuple-element.12, s32[1536]{0:T(1024)S(1)} %get-tuple-element.15, s32[256]{0:T(256)S(1)} %get-tuple-element.18, s32[256]{0:T(256)S(1)} %get-tuple-element.23, ...), kind=kLoop, calls=%fused_computation.23 | loop fusion | flops 10223616 | bytes 818688 | tf_op jit(solution)/shard_map/convert_element_type | solution.py:130
  103.7 0.2 copy.35
  103.8 0.3 pad.12
  104.1 0.3 copy.36
  104.4 1.0 reshape.32
  105.4 1.3 copy.46
  106.7 1.2 pad.14
  107.8 1.2 copy.47.cols
  109.0 0.3 pad_bitcast_fusion
  109.3 0.5 copy.37
  109.8 1.2 copy.42.win
  111.0 17.0 %dress_first.1 = (bf16[2,1344,1344]{2,1,0:T(8,128)(2,1)}, f32[1536,1536]{1,0:T(8,128)}) custom-call(bf16[64,1,84,336]{3,2,1,0:T(8,128)(2,1)} %all_to_all.25.pieces, bf16[256,1536]{1,0:T(8,128)(2,1)} %copy.42.win, bf16[256,1536]{1,0:T(8,128)(2,1)} %copy.47.cols, bf16[1536,256]{1,0:T(8,128)(2,1)} %fusion.15.sel), custom_call_target="tpu_custom_call" | custom-call | tf_op jit(solution)/shard_map/dress_first/pallas_call | solution.py:99
  128.0 25.1 %all-to-all-done.pieces = bf16[64,1,84,336]{3,2,1,0:T(8,128)(2,1)} async-done(((bf16[64,1,84,336]{3,2,1,0:T(8,128)(2,1)}), bf16[64,1,84,336]{3,2,1,0:T(8,128)(2,1)}, u32[]{:S(2)}, u32[]{:S(2)}) %all-to-all-start) | async-done | bytes 3612704 | tf_op jit(solution)/shard_map/all_to_all | solution.py:139
  153.1 18.3 %dress_last.1 = (bf16[2,1344,1344]{2,1,0:T(8,128)(2,1)}, bf16[2,32,84,336]{3,2,1,0:T(8,128)(2,1)}) custom-call(bf16[64,1,84,336]{3,2,1,0:T(8,128)(2,1)} %all-to-all-done.pieces, bf16[256,1536]{1,0:T(8,128)(2,1)} %copy.42.win, bf16[256,1536]{1,0:T(8,128)(2,1)} %copy.47.cols, bf16[1536,256]{1,0:T(8,128)(2,1)} %fusion.15.sel, ...), custom_call_target="tpu_custom_call", output_to_operand_aliasing={{0}: (5, {})} | custom-call | tf_op jit(solution)/shard_map/dress_last/pallas_call | solution.py:99
  171.5 2.8 %copy.43 = bf16[2,32,84,336]{3,1,2,0:T(8,128)(2,1)S(1)} copy(bf16[2,32,84,336]{3,2,1,0:T(8,128)(2,1)} %get-tuple-element.9) | data formatting | bytes 7225344 | tf_op jit(solution)/shard_map/dress_last/pallas_call | solution.py:99
  174.3 8.3 %all_to_all.26 = bf16[2,32,84,336]{3,1,2,0:T(8,128)(2,1)S(1)} all-to-all(bf16[2,32,84,336]{3,1,2,0:T(8,128)(2,1)S(1)} %copy.43), channel_id=1, replica_groups=mesh['pb'=2,'row_0'=4,'row_1'=4,'col_0'=2,'col_1'=2] {'col_1'}, dimensions={0} | all-to-all | bytes 7225344 | tf_op jit(solution)/shard_map/all_to_all | solution.py:139
  182.6 0.6 fusion.4
  183.1 0.7 copy.44
  183.9 38.7 %all_to_all.27 = bf16[32,84,336]{2,1,0:T(8,128)(2,1)S(1)} all-to-all(bf16[32,84,336]{2,1,0:T(8,128)(2,1)S(1)} %copy.44), channel_id=1, replica_groups=mesh['pb'=2,'row_0'=4,'row_1'=4,'col_0'=2,'col_1'=2] {'row_0','row_1','c..., dimensions={0} | all-to-all | bytes 3612672 | tf_op jit(solution)/shard_map/all_to_all | solution.py:139
  222.6 0.4 reduce_sum.12
  222.9 1.1 collective-permute-start
  224.0 3.3 %collective-permute-done = bf16[84,336]{1,0:T(8,128)(2,1)S(1)} collective-permute-done((bf16[84,336]{1,0:T(8,128)(2,1)S(1)}, bf16[84,336]{1,0:T(8,128)(2,1)S(1)}, u32[]{:S(2)}, u32[]{:S(2)}) %collective-permute-start) | collective-permute-done | bytes 56480 | tf_op jit(solution)/shard_map/ppermute | solution.py:158
  227.3 0.7 convert_add_fusion
  (6 shorter events, 0.0 us)
Async XLA Ops:
  2.4 25.1 %all-to-all-start.1 = ((bf16[16,144,75]{2,1,0:T(8,128)(2,1)}), bf16[16,144,75]{2,1,0:T(8,128)(2,1)S(1)}, u32[]{:S(2)}, u32[]{:S(2)}) async-start(bf16[16,144,75]{2,1,0:T(8,128)(2,1)} %broadcast_in_dim.3), calls=%async_computation.1 | async-start | bytes 1179648 | tf_op jit(solution)/shard_map/all_to_all | solution.py:139
  93.9 59.2 %all-to-all-start = ((bf16[64,1,84,336]{3,2,1,0:T(8,128)(2,1)}), bf16[64,1,84,336]{3,2,1,0:T(8,128)(2,1)}, u32[]{:S(2)}, u32[]{:S(2)}) async-start(bf16[64,1,84,336]{3,2,1,0:T(8,128)(2,1)} %get-tuple-element.11), calls=%async_computation | async-start | bytes 8650752 | tf_op jit(solution)/shard_map/all_to_all | solution.py:139
  222.9 4.4 %collective-permute-start = (bf16[84,336]{1,0:T(8,128)(2,1)S(1)}, bf16[84,336]{1,0:T(8,128)(2,1)S(1)}, u32[]{:S(2)}, u32[]{:S(2)}) collective-permute-start(bf16[84,336]{1,0:T(8,128)(2,1)S(1)} %reduce_sum.12), channel_id=1, source_target_pairs={{0,64},{64,0},{1,65},{65,1},{2,66},{66,2},{3,67},{67,3},{4,68},{68... | collective-permute-start | bytes 169352 | tf_op jit(solution)/shard_map/ppermute | solution.py:158

commit v3 on v2

v3 whole, which is shorter than its diff:
```python
import functools

import jax
import jax.numpy as jnp
from jax import lax
from jax.experimental import pallas as pl
from jax.experimental.pallas import tpu as pltpu
from jax.sharding import Mesh
from jax.sharding import PartitionSpec as P

OG, SH = 9, 84
RP, CP, WIN = 96, 384, 16
FULL, LANES, TALL, LONG = 80, 256, 28, 112
VMEM = pl.BlockSpec(memory_space=pltpu.VMEM)
HBM = pl.BlockSpec(memory_space=pltpu.HBM)


def hot(condition):
    return jnp.where(condition, 1.0, 0.0).astype(jnp.bfloat16)


def pack(own, q_own, source, out, held, wire, sem, sent):
    height, width, depth = held.shape
    rest = width - LANES
    devices = depth // q_own
    spans = [(at, min(WIN, height - at)) for at in range(0, height, WIN)]
    copies = [
        pltpu.make_async_copy(source.at[at : at + n], held.at[at : at + n], sem.at[k])
        for k, (at, n) in enumerate(spans)
    ]
    for copy in copies:
        copy.start()
    row = lax.broadcasted_iota(jnp.int32, (devices, depth), 0)
    col = lax.broadcasted_iota(jnp.int32, (devices, depth), 1)
    pick = hot(col == row * q_own + own)
    row = lax.broadcasted_iota(jnp.int32, (LANES, LANES), 0)
    col = lax.broadcasted_iota(jnp.int32, (LANES, LANES), 1)
    turn = hot((row // WIN == col % WIN) & (row % WIN == col // WIN))
    zeros = jnp.zeros((LANES - 3 * rest, depth), jnp.bfloat16)

    def slab(k):
        if k < FULL:
            return held[k, :LANES, :]
        k -= FULL
        if k >= TALL:
            return held[FULL + k - TALL, :LANES, :]
        parts = [held[i * TALL + k, LANES:, :] for i in range(3)]
        return jnp.concatenate(parts + [zeros], axis=0)

    for g in range(LONG // WIN):
        if g < FULL // WIN:
            copies[g].wait()
        elif g == FULL // WIN:
            for copy in copies[g:]:
                copy.wait()
        flat = [
            lax.dot_general(
                pick, slab(g * WIN + k), (((1,), (1,)), ((), ())), preferred_element_type=jnp.float32
            ).astype(jnp.bfloat16)
            for k in range(WIN)
        ]
        for t in range(devices // WIN):
            mixed = jnp.concatenate([f[t * WIN : (t + 1) * WIN] for f in flat], axis=0)
            done = jnp.dot(turn, mixed, preferred_element_type=jnp.float32).astype(jnp.bfloat16)
            done = done.reshape(WIN, WIN, LANES)
            wire[g, t * WIN : (t + 1) * WIN] = done
        pltpu.make_async_copy(wire.at[g], out.at[:, g * WIN : (g + 1) * WIN], sent.at[g]).start()
    for g in range(LONG // WIN):
        pltpu.make_async_copy(wire.at[g], out.at[:, g * WIN : (g + 1) * WIN], sent.at[g]).wait()


def pack_call(own, q_own, source):
    height, _, depth = source.shape
    source = pltpu.with_memory_space_constraint(source, pltpu.HBM)
    return pl.pallas_call(
        functools.partial(pack, own, q_own),
        out_shape=pltpu.HBM((depth // q_own, LONG, LANES), jnp.bfloat16),
        in_specs=[HBM],
        out_specs=HBM,
        scratch_shapes=[
            pltpu.VMEM(source.shape, jnp.bfloat16),
            pltpu.VMEM((LONG // WIN, depth // q_own, WIN, LANES), jnp.bfloat16),
            pltpu.SemaphoreType.DMA((-(-height // WIN),)),
            pltpu.SemaphoreType.DMA((LONG // WIN,)),
        ],
        compiler_params=pltpu.CompilerParams(vmem_limit_bytes=20 * 2**20),
        cost_estimate=pl.CostEstimate(flops=5 * 10**9, bytes_accessed=10**7, transcendentals=0),
        name="pack",
    )(source)


def dress(own, last, pieces, win, cols, sel, *rest):
    if last:
        core, before, _, whole, mine, theirs, held, x, top, stage, hsem, sem, fock, fsem = rest
    else:
        whole, kept, held, x, top, stage, hsem, sem, fock, fsem = rest
    rows = x.shape[0]
    blocks = x.shape[2] // CP
    width = stage.shape[1] // blocks
    side = width - LANES
    per = rows // blocks
    deep, tall = per * RP, per * SH

    def come(m):
        part = pl.ds(m * per * blocks, per * blocks)
        return pltpu.make_async_copy(pieces.at[part], held.at[part], hsem.at[m])

    def leave(m):
        part = pl.ds(m * tall, tall)
        return pltpu.make_async_copy(stage.at[part], whole.at[own, part], sem.at[m])

    def carried(m):
        if last:
            return pltpu.make_async_copy(before.at[m], fock.at[m], fsem.at[m])
        return pltpu.make_async_copy(fock.at[m], kept.at[m], fsem.at[m])

    for m in range(blocks):
        come(m).start()
    if last:
        for m in range(blocks):
            carried(m).start()
    for c in range(blocks):
        x[:, :, c * CP + width : (c + 1) * CP] = jnp.zeros((rows, RP, CP - width), jnp.bfloat16)
    x[:, FULL:, :] = jnp.zeros((rows, RP - FULL, blocks * CP), jnp.bfloat16)

    def place(r, carry):
        for c in range(blocks):
            at = r * blocks + c
            lane = c * CP
            x[r, :FULL, lane : lane + LANES] = held[at, :FULL, :]
            x[r, FULL:SH, lane : lane + LANES] = held[at, FULL + TALL :, :]
            for i in range(3):
                x[r, i * TALL : (i + 1) * TALL, lane + LANES : lane + width] = held[
                    at, FULL : FULL + TALL, i * side : (i + 1) * side
                ]
        return carry

    for m in range(blocks):
        come(m).wait()
        lax.fori_loop(m * per, (m + 1) * per, place, 0)
    flat = x.reshape(rows * RP, blocks * CP)
    shift = jnp.dot(win[...], flat[...], preferred_element_type=jnp.float32)
    for r in range(rows):
        at = slice(r * RP, r * RP + WIN)
        fixed = flat[at, :].astype(jnp.float32) - shift[r * WIN : (r + 1) * WIN]
        flat[at, :] = fixed.astype(jnp.bfloat16)
    g = jnp.dot(flat[...], sel[...], preferred_element_type=jnp.float32).astype(jnp.bfloat16)
    inner = jnp.concatenate([g[r * RP : r * RP + WIN, :] for r in range(rows)], axis=0)
    here = lax.broadcasted_iota(jnp.int32, inner.shape, 0)
    there = lax.broadcasted_iota(jnp.int32, inner.shape, 1)
    weight = 2.0 * jnp.sum(jnp.where(here == there, inner.astype(jnp.float32), 0.0))
    for m in range(blocks):
        at = slice(m * deep, (m + 1) * deep)
        extra = jnp.dot(g[at], cols[...], preferred_element_type=jnp.float32)
        new = (flat[at, :].astype(jnp.float32) + extra).astype(jnp.bfloat16)
        flat[at, :] = new
        for r in range(per):
            for c in range(blocks):
                block = new[r * RP : r * RP + SH, c * CP : c * CP + width]
                down = m * tall + r * SH
                stage[down : down + SH, c * width : (c + 1) * width] = block
            to = (m * per + r) * WIN
            top[to : to + WIN, :] = new[r * RP : r * RP + WIN, :]
        leave(m).start()

    def wired(target, at, block):
        target[at, :FULL, :] = block[:FULL, :LANES]
        target[at, FULL + TALL :, :] = block[FULL:, :LANES]
        for i in range(3):
            target[at, FULL : FULL + TALL, i * side : (i + 1) * side] = block[
                i * TALL : (i + 1) * TALL, LANES:
            ]
        target[at, FULL : FULL + TALL, 3 * side :] = jnp.zeros(
            (TALL, LANES - 3 * side), jnp.bfloat16
        )

    for m in range(blocks):
        at = slice(m * deep, (m + 1) * deep)
        swapped = jnp.dot(g[at], top[...], preferred_element_type=jnp.float32)
        total = weight * flat[at, :].astype(jnp.float32) - swapped
        if not last:
            fock[m] = total
            carried(m).start()
            continue
        odd = core[0] == 1
        carried(m).wait()
        total = (total + fock[m]).astype(jnp.bfloat16)
        for r in range(per):
            for h in range(blocks // 2):
                pair = [
                    total[r * RP : r * RP + SH, c * CP : c * CP + width] for c in (2 * h, 2 * h + 1)
                ]
                to = (m * per + r) * (blocks // 2) + h
                wired(mine, to, jnp.where(odd, pair[1], pair[0]))
                wired(theirs, to, jnp.where(odd, pair[0], pair[1]))
    for m in range(blocks):
        leave(m).wait()
        if not last:
            carried(m).wait()


def dress_call(own, q_own, shape, pieces, win, cols, sel, core=None, before=None, whole=None):
    last = before is not None
    rows, blocks, _ = shape
    norb = rows * SH
    pieces = pltpu.with_memory_space_constraint(pieces, pltpu.HBM)
    half = pltpu.VMEM((rows * blocks // 2, LONG, LANES), jnp.bfloat16)
    split = (blocks, rows // blocks * RP, blocks * CP)
    whole_shape = pltpu.HBM((q_own, norb, norb), jnp.bfloat16)
    if last:
        before = pltpu.with_memory_space_constraint(before, pltpu.HBM)
        args = (pieces, win, cols, sel, core, before, whole)
        in_specs = [HBM, VMEM, VMEM, VMEM, pl.BlockSpec(memory_space=pltpu.SMEM), HBM, HBM]
        out_shape, out_specs = (whole_shape, half, half), (HBM, VMEM, VMEM)
    else:
        args = (pieces, win, cols, sel)
        in_specs = [HBM, VMEM, VMEM, VMEM]
        out_shape = (whole_shape, pltpu.HBM(split, jnp.float32))
        out_specs = (HBM, HBM)
    sem = pltpu.SemaphoreType.DMA((blocks,))
    return pl.pallas_call(
        functools.partial(dress, own, last),
        out_shape=out_shape,
        in_specs=in_specs,
        out_specs=out_specs,
        input_output_aliases={6: 0} if last else {},
        scratch_shapes=[
            pltpu.VMEM(pieces.shape, jnp.bfloat16),
            pltpu.VMEM((rows, RP, blocks * CP), jnp.bfloat16),
            pltpu.VMEM((rows * WIN, blocks * CP), jnp.bfloat16),
            pltpu.VMEM((norb, norb), jnp.bfloat16),
            sem,
            sem,
            pltpu.VMEM(split, jnp.float32),
            sem,
        ],
        compiler_params=pltpu.CompilerParams(vmem_limit_bytes=48 * 2**20),
        cost_estimate=pl.CostEstimate(flops=10**10, bytes_accessed=10**7, transcendentals=0),
        name="dress_last" if last else "dress_first",
    )(*args)


def finish(own, other, fock):
    width = fock.shape[1]
    side = width - LANES
    total = own[...].astype(jnp.float32) + other[...].astype(jnp.float32)
    fock[:FULL, :LANES] = total[:FULL]
    fock[FULL:, :LANES] = total[FULL + TALL :]
    for i in range(3):
        fock[i * TALL : (i + 1) * TALL, LANES:] = total[
            FULL : FULL + TALL, i * side : (i + 1) * side
        ]


def finish_call(own, other, width):
    return pl.pallas_call(
        finish,
        out_shape=jax.ShapeDtypeStruct((SH, width), jnp.float32),
        in_specs=[VMEM] * 2,
        out_specs=VMEM,
        name="finish",
    )(own, other)


def tables(amp, blocks):
    groups = amp.shape[0]
    cut = amp.reshape(groups, groups, OG, SH - OG)
    cut = jnp.pad(cut, ((0, 0), (0, 0), (0, WIN - OG), (OG, 0))).reshape(groups, groups * WIN, SH)
    win = jnp.pad(cut, ((0, 0), (0, 0), (0, RP - SH)))
    win = jnp.transpose(win, (1, 0, 2)).reshape(groups * WIN, groups * RP)
    per = groups // blocks
    cols = jnp.transpose(cut, (1, 0, 2)).reshape(groups * WIN, blocks, per * SH)
    cols = jnp.pad(cols, ((0, 0), (0, 0), (0, CP - per * SH))).reshape(groups * WIN, blocks * CP)
    at = lax.broadcasted_iota(jnp.int32, (blocks * CP, groups * WIN), 0)
    to = lax.broadcasted_iota(jnp.int32, (blocks * CP, groups * WIN), 1)
    inside = at % CP
    group = at // CP * per + inside // SH
    hit = (inside < per * SH) & (to // WIN == group) & (to % WIN == inside % SH) & (inside % SH < OG)
    return win, cols, hit.astype(jnp.bfloat16)


ROW = ("row_0", "row_1")
COL = ("col_0", "col_1")
ALL = (*ROW, *COL)


def swap(array, axis):
    return lax.all_to_all(array, axis, split_axis=0, concat_axis=0, tiled=True)


def all_of(array, axis):
    count = lax.axis_size(axis)
    here = lax.axis_index(axis)
    found = [array]
    for step in range(1, count):
        pairs = [((to + step) % count, to) for to in range(count)]
        found.append(lax.ppermute(array, axis, pairs))
    found = jnp.stack(found + found[:-1])
    return lax.dynamic_slice_in_dim(found, (count - here) % count, count, 0)


def step(chol, amplitudes):
    q_local, _, col_width = chol.shape
    shape = (lax.axis_size(ROW), lax.axis_size(COL), col_width)
    q_own = q_local // lax.axis_size(ALL)
    source = jnp.transpose(chol, (1, 2, 0))
    sent, amplitudes = lax.optimization_barrier((pack_call(0, q_own, source), amplitudes))
    first = swap(sent, ALL)
    amp = all_of(amplitudes, ROW)
    win, into, sel = tables(amp, shape[1])
    second = swap(pack_call(1, q_own, source), ALL)
    core = lax.axis_index("col_1").astype(jnp.int32).reshape(1)
    whole, part = dress_call(0, q_own, shape, first, win, into, sel)
    whole, mine, theirs = dress_call(1, q_own, shape, second, win, into, sel, core, part, whole)
    came = lax.ppermute(theirs, "col_1", ((0, 1), (1, 0)))
    fock = (mine.astype(jnp.float32) + came.astype(jnp.float32)).astype(jnp.bfloat16)
    fock = swap(fock, (*ROW, "col_0"))
    fock = jnp.sum(fock.astype(jnp.float32), axis=0).astype(jnp.bfloat16)
    other = lax.ppermute(fock, "pb", ((0, 1), (1, 0)))
    return whole, finish_call(fock, other, col_width)


def solution(mesh):
    finer = Mesh(
        mesh.devices.reshape(mesh.shape["pb"], 4, 4, mesh.shape["col"] // 2, 2),
        ("pb", *ALL),
    )
    placed = (P("pb", ROW, COL), P(None, ROW))
    return jax.shard_map(
        step,
        mesh=finer,
        in_specs=placed,
        out_specs=(P(("pb", *ALL), None, None), P(ROW, COL)),
        check_vma=False,
    )
```

time: 229 us -> 247 us (1.079)
  blocking collectives: 113 us -> 34.2 us
  waiting for transfers between devices: 28.4 us -> 95.8 us
  starting transfers between devices: 14.5 us -> 63 us
  local copies, waits for them, and re-layouts: 30.5 us -> 5.03 us
  Pallas kernels: 35.3 us -> 44.6 us
    all_to_all x3 -> x1, blocking collectives: 113 us -> 34.2 us  [swap(): return lax.all_to_all(array, axis, split_axis=0, concat_axis=0, tiled=True)]
    ppermute x1 -> x17, waiting for transfers between devices: 3.27 us -> 66.6 us  [the longest x15 60 us: all_of(): found.append(lax.ppermute(array, axis, pairs))]
    ppermute x1 -> x17, starting transfers between devices: 1.1 us -> 43.2 us  [the longest x15 41.2 us: all_of(): found.append(lax.ppermute(array, axis, pairs))]
    unnamed x1 -> x36, local copies, waits for them, and re-layouts: 11.7 us -> 0.94 us
    pallas_call x2 -> x5, Pallas kernels: 35.3 us -> 44.6 us  [the longest x2 27.6 us: dress_call(): pl.pallas_call(functools.partial(dress, own, last), out_shape=out_shape,...]
    all_to_all x2, starting transfers between devices: 13.4 us -> 19.8 us  [swap(): return lax.all_to_all(array, axis, split_axis=0, concat_axis=0, tiled=True)]
    squeeze x1 -> x0, local copies, waits for them, and re-layouts: 6.25 us -> none  [local(): first = swap(sent[:, 0], ALL)]
    all_to_all x2, waiting for transfers between devices: 25.1 us -> 29.2 us  [swap(): return lax.all_to_all(array, axis, split_axis=0, concat_axis=0, tiled=True)]
  transfers between devices with their start and end apart: 3 -> 19, of which waited for: 2 -> 13; matrix products, arithmetic and copies ran while one was open for 13% -> 3% of each run, Pallas kernels for 7% -> 8%
where the time goes in v3:
time: 247 us
  waiting for transfers between devices  95.8 us (39%)
  starting transfers between devices  63 us (26%)
  Pallas kernels  44.6 us (18%)
  blocking collectives  34.2 us (14%)
  local copies, waits for them, and re-layouts  5.03 us (2%)
  other arithmetic  3.11 us (1%)
    ppermute x15, waiting for transfers between devices, all_of(): found.append(lax.ppermute(array, axis, pairs))  60 us
    ppermute x15, starting transfers between devices, all_of(): found.append(lax.ppermute(array, axis, pairs))  41.2 us
    all_to_all x1, blocking collectives, swap(): return lax.all_to_all(array, axis, split_axis=0, concat_axis=0, tiled=True)  34.2 us
    all_to_all x2, waiting for transfers between devices, swap(): return lax.all_to_all(array, axis, split_axis=0, concat_axis=0, tiled=True)  29.2 us
    pallas_call x2, Pallas kernels, dress_call(): pl.pallas_call(functools.partial(dress, own, last), out_shape=out_shape,...  27.6 us
    all_to_all x2, starting transfers between devices, swap(): return lax.all_to_all(array, axis, split_axis=0, concat_axis=0, tiled=True)  19.8 us
    pallas_call x2, Pallas kernels, pack_call(): pl.pallas_call(functools.partial(pack, own, q_own), out_shape=pltpu.HBM((...  15.4 us
  transfers between devices with their start and end apart: 19, of which 13 were waited for; matrix products, arithmetic and copies ran while one was open for 3% of the time, Pallas kernels for 8%

profile of v3, /device:TPU:0, one launch (start us, length us, event | category | flops | bytes accessed | tf_op | source)
XLA Modules:
  0.0 246.8 jit_solution(10525468188023103792)
XLA Ops:
  0.6 7.7 %pack.3 = bf16[64,112,256]{2,1,0:T(8,128)(2,1)} custom-call(bf16[84,336,128]{2,1,0:T(8,128)(2,1)} %bitcast.63), custom_call_target="tpu_custom_call" | custom-call | flops 5000000000 | bytes 10000000 | tf_op jit(solution)/shard_map/pack/pallas_call | solution.py:75
  8.3 1.8 collective-permute-start.14
  10.1 2.9 %collective-permute-start.13 = (bf16[144,75]{1,0:T(8,128)(2,1)S(1)}, bf16[144,75]{1,0:T(8,128)(2,1)S(1)}, u32[]{:S(2)}, u32[]{:S(2)}) collective-permute-start(bf16[144,75]{1,0:T(8,128)(2,1)S(1)} %copy-done.1), channel_id=1, source_target_pairs={{56,0},{60,4},{0,8},{4,12},{8,16},{12,20},{16,24},{20,28},{24,32},... | collective-permute-start | bytes 64808 | tf_op jit(solution)/shard_map/ppermute | solution.py:297
  13.0 2.3 collective-permute-start.12
  15.3 1.5 collective-permute-start.11
  16.8 2.0 collective-permute-start
  18.7 7.8 %all-to-all-start.1 = ((bf16[64,112,256]{2,1,0:T(8,128)(2,1)}), bf16[64,112,256]{2,1,0:T(8,128)(2,1)}, u32[]{:S(2)}, u32[]{:S(2)}) async-start(bf16[64,112,256]{2,1,0:T(8,128)(2,1)} %pack.3), calls=%async_computation.1 | async-start | bytes 7340032 | tf_op jit(solution)/shard_map/all_to_all | solution.py:288
  26.6 7.7 %pack.2 = bf16[64,112,256]{2,1,0:T(8,128)(2,1)} custom-call(bf16[84,336,128]{2,1,0:T(8,128)(2,1)} %bitcast.64), custom_call_target="tpu_custom_call" | custom-call | flops 5000000000 | bytes 10000000 | tf_op jit(solution)/shard_map/pack/pallas_call | solution.py:75
  34.4 2.3 fusion.14.sel
  36.7 5.5 %collective-permute-start.1 = (bf16[144,75]{1,0:T(8,128)(2,1)S(1)}, bf16[144,75]{1,0:T(8,128)(2,1)S(1)}, u32[]{:S(2)}, u32[]{:S(2)}) collective-permute-start(bf16[144,75]{1,0:T(8,128)(2,1)S(1)} %copy-done.1), channel_id=1, source_target_pairs={{8,0},{12,4},{16,8},{20,12},{24,16},{28,20},{32,24},{36,28},{40,32... | collective-permute-start | bytes 64808 | tf_op jit(solution)/shard_map/ppermute | solution.py:297
  42.1 30.5 %collective-permute-done.1 = bf16[144,75]{1,0:T(8,128)(2,1)S(1)} collective-permute-done((bf16[144,75]{1,0:T(8,128)(2,1)S(1)}, bf16[144,75]{1,0:T(8,128)(2,1)S(1)}, u32[]{:S(2)}, u32[]{:S(2)}) %collective-permute-start.1) | collective-permute-done | bytes 21632 | tf_op jit(solution)/shard_map/ppermute | solution.py:297
  72.6 2.0 collective-permute-start.2
  74.6 3.1 %collective-permute-done.2 = bf16[144,75]{1,0:T(8,128)(2,1)S(1)} collective-permute-done((bf16[144,75]{1,0:T(8,128)(2,1)S(1)}, bf16[144,75]{1,0:T(8,128)(2,1)S(1)}, u32[]{:S(2)}, u32[]{:S(2)}) %collective-permute-start.2) | collective-permute-done | bytes 21632 | tf_op jit(solution)/shard_map/ppermute | solution.py:297
  77.8 1.7 collective-permute-start.3
  79.5 2.2 collective-permute-done.3
  81.7 2.3 collective-permute-start.4
  84.0 2.6 %collective-permute-done.4 = bf16[144,75]{1,0:T(8,128)(2,1)S(1)} collective-permute-done((bf16[144,75]{1,0:T(8,128)(2,1)S(1)}, bf16[144,75]{1,0:T(8,128)(2,1)S(1)}, u32[]{:S(2)}, u32[]{:S(2)}) %collective-permute-start.4) | collective-permute-done | bytes 21632 | tf_op jit(solution)/shard_map/ppermute | solution.py:297
  86.6 2.2 collective-permute-start.5
  88.8 4.2 %collective-permute-done.5 = bf16[144,75]{1,0:T(8,128)(2,1)S(1)} collective-permute-done((bf16[144,75]{1,0:T(8,128)(2,1)S(1)}, bf16[144,75]{1,0:T(8,128)(2,1)S(1)}, u32[]{:S(2)}, u32[]{:S(2)}) %collective-permute-start.5) | collective-permute-done | bytes 21632 | tf_op jit(solution)/shard_map/ppermute | solution.py:297
  93.0 2.8 %collective-permute-start.6 = (bf16[144,75]{1,0:T(8,128)(2,1)S(1)}, bf16[144,75]{1,0:T(8,128)(2,1)S(1)}, u32[]{:S(2)}, u32[]{:S(2)}) collective-permute-start(bf16[144,75]{1,0:T(8,128)(2,1)S(1)} %copy-done.1), channel_id=1, source_target_pairs={{28,0},{32,4},{36,8},{40,12},{44,16},{48,20},{52,24},{56,28},{60,3... | collective-permute-start | bytes 64808 | tf_op jit(solution)/shard_map/ppermute | solution.py:297
  95.7 3.7 %collective-permute-done.6 = bf16[144,75]{1,0:T(8,128)(2,1)S(1)} collective-permute-done((bf16[144,75]{1,0:T(8,128)(2,1)S(1)}, bf16[144,75]{1,0:T(8,128)(2,1)S(1)}, u32[]{:S(2)}, u32[]{:S(2)}) %collective-permute-start.6) | collective-permute-done | bytes 21632 | tf_op jit(solution)/shard_map/ppermute | solution.py:297
  99.5 4.3 %collective-permute-start.7 = (bf16[144,75]{1,0:T(8,128)(2,1)S(1)}, bf16[144,75]{1,0:T(8,128)(2,1)S(1)}, u32[]{:S(2)}, u32[]{:S(2)}) collective-permute-start(bf16[144,75]{1,0:T(8,128)(2,1)S(1)} %copy-done.1), channel_id=1, source_target_pairs={{32,0},{36,4},{40,8},{44,12},{48,16},{52,20},{56,24},{60,28},{0,32... | collective-permute-start | bytes 64808 | tf_op jit(solution)/shard_map/ppermute | solution.py:297
  103.8 1.9 collective-permute-done.7
  105.7 3.6 %collective-permute-start.8 = (bf16[144,75]{1,0:T(8,128)(2,1)S(1)}, bf16[144,75]{1,0:T(8,128)(2,1)S(1)}, u32[]{:S(2)}, u32[]{:S(2)}) collective-permute-start(bf16[144,75]{1,0:T(8,128)(2,1)S(1)} %copy-done.1), channel_id=1, source_target_pairs={{36,0},{40,4},{44,8},{48,12},{52,16},{56,20},{60,24},{0,28},{4,32}... | collective-permute-start | bytes 64808 | tf_op jit(solution)/shard_map/ppermute | solution.py:297
  109.4 2.7 %collective-permute-done.8 = bf16[144,75]{1,0:T(8,128)(2,1)S(1)} collective-permute-done((bf16[144,75]{1,0:T(8,128)(2,1)S(1)}, bf16[144,75]{1,0:T(8,128)(2,1)S(1)}, u32[]{:S(2)}, u32[]{:S(2)}) %collective-permute-start.8) | collective-permute-done | bytes 21632 | tf_op jit(solution)/shard_map/ppermute | solution.py:297
  112.1 3.7 %collective-permute-start.9 = (bf16[144,75]{1,0:T(8,128)(2,1)S(1)}, bf16[144,75]{1,0:T(8,128)(2,1)S(1)}, u32[]{:S(2)}, u32[]{:S(2)}) collective-permute-start(bf16[144,75]{1,0:T(8,128)(2,1)S(1)} %copy-done.1), channel_id=1, source_target_pairs={{40,0},{44,4},{48,8},{52,12},{56,16},{60,20},{0,24},{4,28},{8,32},... | collective-permute-start | bytes 64808 | tf_op jit(solution)/shard_map/ppermute | solution.py:297
  115.8 4.3 %collective-permute-done.9 = bf16[144,75]{1,0:T(8,128)(2,1)S(1)} collective-permute-done((bf16[144,75]{1,0:T(8,128)(2,1)S(1)}, bf16[144,75]{1,0:T(8,128)(2,1)S(1)}, u32[]{:S(2)}, u32[]{:S(2)}) %collective-permute-start.9) | collective-permute-done | bytes 21632 | tf_op jit(solution)/shard_map/ppermute | solution.py:297
  120.1 2.8 %collective-permute-start.10 = (bf16[144,75]{1,0:T(8,128)(2,1)S(1)}, bf16[144,75]{1,0:T(8,128)(2,1)S(1)}, u32[]{:S(2)}, u32[]{:S(2)}) collective-permute-start(bf16[144,75]{1,0:T(8,128)(2,1)S(1)} %copy-done.1), channel_id=1, source_target_pairs={{44,0},{48,4},{52,8},{56,12},{60,16},{0,20},{4,24},{8,28},{12,32},... | collective-permute-start | bytes 64808 | tf_op jit(solution)/shard_map/ppermute | solution.py:297
  122.9 4.8 %collective-permute-done.10 = bf16[144,75]{1,0:T(8,128)(2,1)S(1)} collective-permute-done((bf16[144,75]{1,0:T(8,128)(2,1)S(1)}, bf16[144,75]{1,0:T(8,128)(2,1)S(1)}, u32[]{:S(2)}, u32[]{:S(2)}) %collective-permute-start.10) | collective-permute-done | bytes 21632 | tf_op jit(solution)/shard_map/ppermute | solution.py:297
  127.8 12.0 %all-to-all-start = ((bf16[64,112,256]{2,1,0:T(8,128)(2,1)}), bf16[64,112,256]{2,1,0:T(8,128)(2,1)}, u32[]{:S(2)}, u32[]{:S(2)}) async-start(bf16[64,112,256]{2,1,0:T(8,128)(2,1)} %pack.2), calls=%async_computation | async-start | bytes 7340032 | tf_op jit(solution)/shard_map/all_to_all | solution.py:288
  140.2 0.3 pad.12
  140.5 0.9 copy.11
  141.4 1.0 reshape.25
  142.4 1.2 pad.14
  143.6 0.3 copy.16.cols
  143.8 0.3 copy.15.win
  144.1 13.1 %dress_first.1 = (bf16[2,1344,1344]{2,1,0:T(8,128)(2,1)}, f32[4,384,1536]{2,1,0:T(8,128)}) custom-call(bf16[64,112,256]{2,1,0:T(8,128)(2,1)} %all-to-all-done.1.pieces, bf16[256,1536]{1,0:T(8,128)(2,1)S(1)} %copy.15.win, bf16[256,1536]{1,0:T(8,128)(2,1)S(1)} %copy.16.cols, bf16[1536,256]{1,0:T(8,128)(2,1)S(1)} %fusion.14.sel), custom_call_target="tpu_custom_call" | custom-call | flops 10000000000 | bytes 10000000 | tf_op jit(solution)/shard_map/dress_first/pallas_call | solution.py:221
  157.2 29.2 %all-to-all-done.pieces = bf16[64,112,256]{2,1,0:T(8,128)(2,1)} async-done(((bf16[64,112,256]{2,1,0:T(8,128)(2,1)}), bf16[64,112,256]{2,1,0:T(8,128)(2,1)}, u32[]{:S(2)}, u32[]{:S(2)}) %all-to-all-start) | async-done | bytes 3670048 | tf_op jit(solution)/shard_map/all_to_all | solution.py:288
  186.4 14.5 %dress_last.1 = (bf16[2,1344,1344]{2,1,0:T(8,128)(2,1)}, bf16[32,112,256]{2,1,0:T(8,128)(2,1)S(1)}, bf16[32,112,256]{2,1,0:T(8,128)(2,1)S(1)}) custom-call(bf16[64,112,256]{2,1,0:T(8,128)(2,1)} %all-to-all-done.pieces, bf16[256,1536]{1,0:T(8,128)(2,1)S(1)} %copy.15.win, bf16[256,1536]{1,0:T(8,128)(2,1)S(1)} %copy.16.cols, ...), custom_call_target="tpu_custom_call", output_to_operand_aliasing={{0}: (6, {})} | custom-call | flops 10000000000 | bytes 10000000 | tf_op jit(solution)/shard_map/dress_last/pallas_call | solution.py:221
  201.0 0.9 collective-permute-start.15
  201.8 3.4 %collective-permute-done.15 = bf16[32,112,256]{2,1,0:T(8,128)(2,1)S(1)} collective-permute-done((bf16[32,112,256]{2,1,0:T(8,128)(2,1)S(1)}, bf16[32,112,256]{2,1,0:T(8,128)(2,1)S(1)}, u32[]{:S(2)}, u32[]{:S(2)}) %collective-permute-start.15) | collective-permute-done | bytes 1835040 | tf_op jit(solution)/shard_map/ppermute | solution.py:315
  205.2 0.5 add_convert_fusion
  205.8 34.2 %all_to_all.15 = bf16[32,112,256]{2,1,0:T(8,128)(2,1)S(1)} all-to-all(bf16[32,112,256]{2,1,0:T(8,128)(2,1)S(1)} %add_convert_fusion), channel_id=1, replica_groups=mesh['pb'=2,'row_0'=4,'row_1'=4,'col_0'=2,'col_1'=2] {'row_0','row_1','c..., dimensions={0} | all-to-all | bytes 3670016 | tf_op jit(solution)/shard_map/all_to_all | solution.py:288
  240.0 0.3 reduce_sum.12.own
  240.3 1.1 collective-permute-start.16
  241.4 3.2 %collective-permute-done.16.other = bf16[112,256]{1,0:T(8,128)(2,1)S(1)} collective-permute-done((bf16[112,256]{1,0:T(8,128)(2,1)S(1)}, bf16[112,256]{1,0:T(8,128)(2,1)S(1)}, u32[]{:S(2)}, u32[]{:S(2)}) %collective-permute-start.16) | collective-permute-done | bytes 57376 | tf_op jit(solution)/shard_map/ppermute | solution.py:319
  244.6 0.6 copy-done.2
  245.2 1.6 finish.1
  (51 shorter events, 0.7 us)
Async XLA Ops:
  0.6 7.7 %copy-start.1 = (bf16[144,75]{1,0:T(8,128)(2,1)S(1)}, bf16[144,75]{1,0:T(8,128)(2,1)}, u32[]{:S(2)}) copy-start(bf16[144,75]{1,0:T(8,128)(2,1)} %param.3) | copy-start | bytes 64804
  8.3 119.4 %collective-permute-start.14 = (bf16[144,75]{1,0:T(8,128)(2,1)S(1)}, bf16[144,75]{1,0:T(8,128)(2,1)S(1)}, u32[]{:S(2)}, u32[]{:S(2)}) collective-permute-start(bf16[144,75]{1,0:T(8,128)(2,1)S(1)} %copy-done.1), channel_id=1, source_target_pairs={{60,0},{0,4},{4,8},{8,12},{12,16},{16,20},{20,24},{24,28},{28,32},... | collective-permute-start | bytes 64808 | tf_op jit(solution)/shard_map/ppermute | solution.py:297
  10.1 117.6 %collective-permute-start.13 = (bf16[144,75]{1,0:T(8,128)(2,1)S(1)}, bf16[144,75]{1,0:T(8,128)(2,1)S(1)}, u32[]{:S(2)}, u32[]{:S(2)}) collective-permute-start(bf16[144,75]{1,0:T(8,128)(2,1)S(1)} %copy-done.1), channel_id=1, source_target_pairs={{56,0},{60,4},{0,8},{4,12},{8,16},{12,20},{16,24},{20,28},{24,32},... | collective-permute-start | bytes 64808 | tf_op jit(solution)/shard_map/ppermute | solution.py:297
  13.0 114.7 %collective-permute-start.12 = (bf16[144,75]{1,0:T(8,128)(2,1)S(1)}, bf16[144,75]{1,0:T(8,128)(2,1)S(1)}, u32[]{:S(2)}, u32[]{:S(2)}) collective-permute-start(bf16[144,75]{1,0:T(8,128)(2,1)S(1)} %copy-done.1), channel_id=1, source_target_pairs={{52,0},{56,4},{60,8},{0,12},{4,16},{8,20},{12,24},{16,28},{20,32},... | collective-permute-start | bytes 64808 | tf_op jit(solution)/shard_map/ppermute | solution.py:297
  15.3 112.4 %collective-permute-start.11 = (bf16[144,75]{1,0:T(8,128)(2,1)S(1)}, bf16[144,75]{1,0:T(8,128)(2,1)S(1)}, u32[]{:S(2)}, u32[]{:S(2)}) collective-permute-start(bf16[144,75]{1,0:T(8,128)(2,1)S(1)} %copy-done.1), channel_id=1, source_target_pairs={{48,0},{52,4},{56,8},{60,12},{0,16},{4,20},{8,24},{12,28},{16,32},... | collective-permute-start | bytes 64808 | tf_op jit(solution)/shard_map/ppermute | solution.py:297
  16.8 19.9 %collective-permute-start = (bf16[144,75]{1,0:T(8,128)(2,1)S(1)}, bf16[144,75]{1,0:T(8,128)(2,1)S(1)}, u32[]{:S(2)}, u32[]{:S(2)}) collective-permute-start(bf16[144,75]{1,0:T(8,128)(2,1)S(1)} %copy-done.1), channel_id=1, source_target_pairs={{4,0},{8,4},{12,8},{16,12},{20,16},{24,20},{28,24},{32,28},{36,32}... | collective-permute-start | bytes 64808 | tf_op jit(solution)/shard_map/ppermute | solution.py:297
  18.7 109.1 %all-to-all-start.1 = ((bf16[64,112,256]{2,1,0:T(8,128)(2,1)}), bf16[64,112,256]{2,1,0:T(8,128)(2,1)}, u32[]{:S(2)}, u32[]{:S(2)}) async-start(bf16[64,112,256]{2,1,0:T(8,128)(2,1)} %pack.3), calls=%async_computation.1 | async-start | bytes 7340032 | tf_op jit(solution)/shard_map/all_to_all | solution.py:288
  36.7 35.9 %collective-permute-start.1 = (bf16[144,75]{1,0:T(8,128)(2,1)S(1)}, bf16[144,75]{1,0:T(8,128)(2,1)S(1)}, u32[]{:S(2)}, u32[]{:S(2)}) collective-permute-start(bf16[144,75]{1,0:T(8,128)(2,1)S(1)} %copy-done.1), channel_id=1, source_target_pairs={{8,0},{12,4},{16,8},{20,12},{24,16},{28,20},{32,24},{36,28},{40,32... | collective-permute-start | bytes 64808 | tf_op jit(solution)/shard_map/ppermute | solution.py:297
  72.6 5.2 %collective-permute-start.2 = (bf16[144,75]{1,0:T(8,128)(2,1)S(1)}, bf16[144,75]{1,0:T(8,128)(2,1)S(1)}, u32[]{:S(2)}, u32[]{:S(2)}) collective-permute-start(bf16[144,75]{1,0:T(8,128)(2,1)S(1)} %copy-done.1), channel_id=1, source_target_pairs={{12,0},{16,4},{20,8},{24,12},{28,16},{32,20},{36,24},{40,28},{44,3... | collective-permute-start | bytes 64808 | tf_op jit(solution)/shard_map/ppermute | solution.py:297
  77.8 4.0 %collective-permute-start.3 = (bf16[144,75]{1,0:T(8,128)(2,1)S(1)}, bf16[144,75]{1,0:T(8,128)(2,1)S(1)}, u32[]{:S(2)}, u32[]{:S(2)}) collective-permute-start(bf16[144,75]{1,0:T(8,128)(2,1)S(1)} %copy-done.1), channel_id=1, source_target_pairs={{16,0},{20,4},{24,8},{28,12},{32,16},{36,20},{40,24},{44,28},{48,3... | collective-permute-start | bytes 64808 | tf_op jit(solution)/shard_map/ppermute | solution.py:297
  81.7 4.9 %collective-permute-start.4 = (bf16[144,75]{1,0:T(8,128)(2,1)S(1)}, bf16[144,75]{1,0:T(8,128)(2,1)S(1)}, u32[]{:S(2)}, u32[]{:S(2)}) collective-permute-start(bf16[144,75]{1,0:T(8,128)(2,1)S(1)} %copy-done.1), channel_id=1, source_target_pairs={{20,0},{24,4},{28,8},{32,12},{36,16},{40,20},{44,24},{48,28},{52,3... | collective-permute-start | bytes 64808 | tf_op jit(solution)/shard_map/ppermute | solution.py:297
  86.6 6.4 %collective-permute-start.5 = (bf16[144,75]{1,0:T(8,128)(2,1)S(1)}, bf16[144,75]{1,0:T(8,128)(2,1)S(1)}, u32[]{:S(2)}, u32[]{:S(2)}) collective-permute-start(bf16[144,75]{1,0:T(8,128)(2,1)S(1)} %copy-done.1), channel_id=1, source_target_pairs={{24,0},{28,4},{32,8},{36,12},{40,16},{44,20},{48,24},{52,28},{56,3... | collective-permute-start | bytes 64808 | tf_op jit(solution)/shard_map/ppermute | solution.py:297
  93.0 6.5 %collective-permute-start.6 = (bf16[144,75]{1,0:T(8,128)(2,1)S(1)}, bf16[144,75]{1,0:T(8,128)(2,1)S(1)}, u32[]{:S(2)}, u32[]{:S(2)}) collective-permute-start(bf16[144,75]{1,0:T(8,128)(2,1)S(1)} %copy-done.1), channel_id=1, source_target_pairs={{28,0},{32,4},{36,8},{40,12},{44,16},{48,20},{52,24},{56,28},{60,3... | collective-permute-start | bytes 64808 | tf_op jit(solution)/shard_map/ppermute | solution.py:297
  99.5 6.2 %collective-permute-start.7 = (bf16[144,75]{1,0:T(8,128)(2,1)S(1)}, bf16[144,75]{1,0:T(8,128)(2,1)S(1)}, u32[]{:S(2)}, u32[]{:S(2)}) collective-permute-start(bf16[144,75]{1,0:T(8,128)(2,1)S(1)} %copy-done.1), channel_id=1, source_target_pairs={{32,0},{36,4},{40,8},{44,12},{48,16},{52,20},{56,24},{60,28},{0,32... | collective-permute-start | bytes 64808 | tf_op jit(solution)/shard_map/ppermute | solution.py:297
  105.7 6.4 %collective-permute-start.8 = (bf16[144,75]{1,0:T(8,128)(2,1)S(1)}, bf16[144,75]{1,0:T(8,128)(2,1)S(1)}, u32[]{:S(2)}, u32[]{:S(2)}) collective-permute-start(bf16[144,75]{1,0:T(8,128)(2,1)S(1)} %copy-done.1), channel_id=1, source_target_pairs={{36,0},{40,4},{44,8},{48,12},{52,16},{56,20},{60,24},{0,28},{4,32}... | collective-permute-start | bytes 64808 | tf_op jit(solution)/shard_map/ppermute | solution.py:297
  112.1 8.0 %collective-permute-start.9 = (bf16[144,75]{1,0:T(8,128)(2,1)S(1)}, bf16[144,75]{1,0:T(8,128)(2,1)S(1)}, u32[]{:S(2)}, u32[]{:S(2)}) collective-permute-start(bf16[144,75]{1,0:T(8,128)(2,1)S(1)} %copy-done.1), channel_id=1, source_target_pairs={{40,0},{44,4},{48,8},{52,12},{56,16},{60,20},{0,24},{4,28},{8,32},... | collective-permute-start | bytes 64808 | tf_op jit(solution)/shard_map/ppermute | solution.py:297
  120.1 7.6 %collective-permute-start.10 = (bf16[144,75]{1,0:T(8,128)(2,1)S(1)}, bf16[144,75]{1,0:T(8,128)(2,1)S(1)}, u32[]{:S(2)}, u32[]{:S(2)}) collective-permute-start(bf16[144,75]{1,0:T(8,128)(2,1)S(1)} %copy-done.1), channel_id=1, source_target_pairs={{44,0},{48,4},{52,8},{56,12},{60,16},{0,20},{4,24},{8,28},{12,32},... | collective-permute-start | bytes 64808 | tf_op jit(solution)/shard_map/ppermute | solution.py:297
  127.8 58.6 %all-to-all-start = ((bf16[64,112,256]{2,1,0:T(8,128)(2,1)}), bf16[64,112,256]{2,1,0:T(8,128)(2,1)}, u32[]{:S(2)}, u32[]{:S(2)}) async-start(bf16[64,112,256]{2,1,0:T(8,128)(2,1)} %pack.2), calls=%async_computation | async-start | bytes 7340032 | tf_op jit(solution)/shard_map/all_to_all | solution.py:288
  201.0 4.3 %collective-permute-start.15 = (bf16[32,112,256]{2,1,0:T(8,128)(2,1)S(1)}, bf16[32,112,256]{2,1,0:T(8,128)(2,1)S(1)}, u32[]{:S(2)}, u32[]{:S(2)}) collective-permute-start(bf16[32,112,256]{2,1,0:T(8,128)(2,1)S(1)} %get-tuple-element.15), channel_id=1, source_target_pairs={{0,1},{1,0},{2,3},{3,2},{4,5},{5,4},{6,7},{7,6},{8,9},{9,8},{10,11... | collective-permute-start | bytes 5505032 | tf_op jit(solution)/shard_map/ppermute | solution.py:315
  240.3 4.3 %copy-start = (bf16[112,256]{1,0:T(8,128)(2,1)}, bf16[112,256]{1,0:T(8,128)(2,1)S(1)}, u32[]{:S(2)}) copy-start(bf16[112,256]{1,0:T(8,128)(2,1)S(1)} %reduce_sum.12.own) | copy-start | bytes 172036
  240.3 4.3 %collective-permute-start.16 = (bf16[112,256]{1,0:T(8,128)(2,1)S(1)}, bf16[112,256]{1,0:T(8,128)(2,1)S(1)}, u32[]{:S(2)}, u32[]{:S(2)}) collective-permute-start(bf16[112,256]{1,0:T(8,128)(2,1)S(1)} %reduce_sum.12.own), channel_id=1, source_target_pairs={{0,64},{64,0},{1,65},{65,1},{2,66},{66,2},{3,67},{67,3},{4,68},{68... | collective-permute-start | bytes 172040 | tf_op jit(solution)/shard_map/ppermute | solution.py:319
  244.6 0.6 copy-start.2

commit v4 on v3

--- a/solution.py
+++ b/solution.py
@@ -179,12 +179,12 @@
         swapped = jnp.dot(g[at], top[...], preferred_element_type=jnp.float32)
         total = weight * flat[at, :].astype(jnp.float32) - swapped
         if not last:
-            fock[m] = total
+            fock[m] = total.astype(jnp.bfloat16)
             carried(m).start()
             continue
         odd = core[0] == 1
         carried(m).wait()
-        total = (total + fock[m]).astype(jnp.bfloat16)
+        total = (total + fock[m].astype(jnp.float32)).astype(jnp.bfloat16)
         for r in range(per):
             for h in range(blocks // 2):
                 pair = [
@@ -215,7 +215,7 @@
     else:
         args = (pieces, win, cols, sel)
         in_specs = [HBM, VMEM, VMEM, VMEM]
-        out_shape = (whole_shape, pltpu.HBM(split, jnp.float32))
+        out_shape = (whole_shape, pltpu.HBM(split, jnp.bfloat16))
         out_specs = (HBM, HBM)
     sem = pltpu.SemaphoreType.DMA((blocks,))
     return pl.pallas_call(
@@ -231,7 +231,7 @@
             pltpu.VMEM((norb, norb), jnp.bfloat16),
             sem,
             sem,
-            pltpu.VMEM(split, jnp.float32),
+            pltpu.VMEM(split, jnp.bfloat16),
             sem,
         ],
         compiler_params=pltpu.CompilerParams(vmem_limit_bytes=48 * 2**20),
@@ -253,6 +253,8 @@
 
 
 def finish_call(own, other, width):
+    own = pltpu.with_memory_space_constraint(own, pltpu.VMEM)
+    other = pltpu.with_memory_space_constraint(other, pltpu.VMEM)
     return pl.pallas_call(
         finish,
         out_shape=jax.ShapeDtypeStruct((SH, width), jnp.float32),
@@ -260,6 +262,22 @@
         out_specs=VMEM,
         name="finish",
     )(own, other)
+
+
+def join(here, *refs):
+    count = len(refs) - 1
+    for step in range(count):
+        refs[-1][lax.rem(here[0] + step, count)] = refs[step][...]
+
+
+def join_call(here, parts):
+    return pl.pallas_call(
+        join,
+        out_shape=jax.ShapeDtypeStruct((len(parts), *parts[0].shape), parts[0].dtype),
+        in_specs=[pl.BlockSpec(memory_space=pltpu.SMEM)] + [VMEM] * len(parts),
+        out_specs=VMEM,
+        name="join",
+    )(here, *parts)
 
 
 def tables(amp, blocks):
@@ -295,8 +313,7 @@
     for step in range(1, count):
         pairs = [((to + step) % count, to) for to in range(count)]
         found.append(lax.ppermute(array, axis, pairs))
-    found = jnp.stack(found + found[:-1])
-    return lax.dynamic_slice_in_dim(found, (count - here) % count, count, 0)
+    return join_call(here.astype(jnp.int32).reshape(1), found)
 
 
 def step(chol, amplitudes):

time: 247 us -> 224 us (0.907)
  waiting for transfers between devices: 95.8 us -> 83.1 us
  starting transfers between devices: 63 us -> 50.9 us
  blocking collectives: 34.2 us -> 37.1 us
    ppermute x15, waiting for transfers between devices: 60 us -> 37.3 us  [all_of(): found.append(lax.ppermute(array, axis, pairs))]
    ppermute x15, starting transfers between devices: 41.2 us -> 30.2 us  [all_of(): found.append(lax.ppermute(array, axis, pairs))]
    all_to_all x2, waiting for transfers between devices: 29.2 us -> 38.9 us  [swap(): return lax.all_to_all(array, axis, split_axis=0, concat_axis=0, tiled=True)]
    pallas_call x2, Pallas kernels: 27.6 us -> 24.7 us  [dress_call(): pl.pallas_call(functools.partial(dress, own, last), out_shape=out_shape,...]
    all_to_all x1, blocking collectives: 34.2 us -> 37.1 us  [swap(): return lax.all_to_all(array, axis, split_axis=0, concat_axis=0, tiled=True)]
  transfers between devices with their start and end apart: 19 -> 19, of which waited for: 13 -> 5; matrix products, arithmetic and copies ran while one was open for 3% -> 3% of each run, Pallas kernels for 8% -> 9%
where the time goes in v4:
time: 224 us
  waiting for transfers between devices  83.1 us (37%)
  starting transfers between devices  50.9 us (23%)
  Pallas kernels  42.8 us (19%)
  blocking collectives  37.1 us (17%)
  local copies, waits for them, and re-layouts  5.67 us (3%)
  other arithmetic  3.07 us (1%)
    all_to_all x2, waiting for transfers between devices, swap(): return lax.all_to_all(array, axis, split_axis=0, concat_axis=0, tiled=True)  38.9 us
    ppermute x15, waiting for transfers between devices, all_of(): found.append(lax.ppermute(array, axis, pairs))  37.3 us
    all_to_all x1, blocking collectives, swap(): return lax.all_to_all(array, axis, split_axis=0, concat_axis=0, tiled=True)  37.1 us
    ppermute x15, starting transfers between devices, all_of(): found.append(lax.ppermute(array, axis, pairs))  30.2 us
    pallas_call x2, Pallas kernels, dress_call(): pl.pallas_call(functools.partial(dress, own, last), out_shape=out_shape,...  24.7 us
    all_to_all x2, starting transfers between devices, swap(): return lax.all_to_all(array, axis, split_axis=0, concat_axis=0, tiled=True)  19.5 us
    pallas_call x2, Pallas kernels, pack_call(): pl.pallas_call(functools.partial(pack, own, q_own), out_shape=pltpu.HBM((...  15.4 us
  transfers between devices with their start and end apart: 19, of which 5 were waited for; matrix products, arithmetic and copies ran while one was open for 3% of the time, Pallas kernels for 9%

profile of v4, /device:TPU:0, one launch (start us, length us, event | category | flops | bytes accessed | tf_op | source)
XLA Modules:
  0.0 223.6 jit_solution(3803332440806597230)
XLA Ops:
  0.6 7.7 %pack.3 = bf16[64,112,256]{2,1,0:T(8,128)(2,1)} custom-call(bf16[84,336,128]{2,1,0:T(8,128)(2,1)} %bitcast.17), custom_call_target="tpu_custom_call" | custom-call | flops 5000000000 | bytes 10000000 | tf_op jit(solution)/shard_map/pack/pallas_call | solution.py:75
  8.3 11.6 %all-to-all-start.1 = ((bf16[64,112,256]{2,1,0:T(8,128)(2,1)}), bf16[64,112,256]{2,1,0:T(8,128)(2,1)}, u32[]{:S(2)}, u32[]{:S(2)}) async-start(bf16[64,112,256]{2,1,0:T(8,128)(2,1)} %pack.3), calls=%async_computation.1 | async-start | bytes 7340032 | tf_op jit(solution)/shard_map/all_to_all | solution.py:306
  19.9 7.7 %pack.2 = bf16[64,112,256]{2,1,0:T(8,128)(2,1)} custom-call(bf16[84,336,128]{2,1,0:T(8,128)(2,1)} %bitcast.18), custom_call_target="tpu_custom_call" | custom-call | flops 5000000000 | bytes 10000000 | tf_op jit(solution)/shard_map/pack/pallas_call | solution.py:75
  27.7 0.0 copy-start
  27.7 38.9 %all-to-all-done.1.pieces = bf16[64,112,256]{2,1,0:T(8,128)(2,1)} async-done(((bf16[64,112,256]{2,1,0:T(8,128)(2,1)}), bf16[64,112,256]{2,1,0:T(8,128)(2,1)}, u32[]{:S(2)}, u32[]{:S(2)}) %all-to-all-start.1) | async-done | bytes 3670048 | tf_op jit(solution)/shard_map/all_to_all | solution.py:306
  66.6 7.9 %all-to-all-start = ((bf16[64,112,256]{2,1,0:T(8,128)(2,1)}), bf16[64,112,256]{2,1,0:T(8,128)(2,1)}, u32[]{:S(2)}, u32[]{:S(2)}) async-start(bf16[64,112,256]{2,1,0:T(8,128)(2,1)} %pack.2), calls=%async_computation | async-start | bytes 7340032 | tf_op jit(solution)/shard_map/all_to_all | solution.py:306
  74.5 1.6 collective-permute-start.14
  76.1 2.7 %collective-permute-start.13 = (bf16[144,75]{1,0:T(8,128)(2,1)S(1)}, bf16[144,75]{1,0:T(8,128)(2,1)S(1)}, u32[]{:S(2)}, u32[]{:S(2)}) collective-permute-start(bf16[144,75]{1,0:T(8,128)(2,1)S(1)} %copy-done), channel_id=1, source_target_pairs={{56,0},{60,4},{0,8},{4,12},{8,16},{12,20},{16,24},{20,28},{24,32},... | collective-permute-start | bytes 64808 | tf_op jit(solution)/shard_map/ppermute | solution.py:315
  78.8 2.4 %collective-permute-start.12 = (bf16[144,75]{1,0:T(8,128)(2,1)S(1)}, bf16[144,75]{1,0:T(8,128)(2,1)S(1)}, u32[]{:S(2)}, u32[]{:S(2)}) collective-permute-start(bf16[144,75]{1,0:T(8,128)(2,1)S(1)} %copy-done), channel_id=1, source_target_pairs={{52,0},{56,4},{60,8},{0,12},{4,16},{8,20},{12,24},{16,28},{20,32},... | collective-permute-start | bytes 64808 | tf_op jit(solution)/shard_map/ppermute | solution.py:315
  81.2 1.6 collective-permute-start.11
  82.7 1.3 collective-permute-start.10
  84.1 36.8 %collective-permute-done.14.refs_15_ = bf16[144,75]{1,0:T(8,128)(2,1)S(1)} collective-permute-done((bf16[144,75]{1,0:T(8,128)(2,1)S(1)}, bf16[144,75]{1,0:T(8,128)(2,1)S(1)}, u32[]{:S(2)}, u32[]{:S(2)}) %collective-permute-start.14) | collective-permute-done | bytes 21632 | tf_op jit(solution)/shard_map/ppermute | solution.py:315
  120.9 0.4 collective-permute-start.9
  121.4 0.0 collective-permute-done.13.refs_14_
  121.4 1.4 collective-permute-start.8
  122.8 4.0 %collective-permute-start.7 = (bf16[144,75]{1,0:T(8,128)(2,1)S(1)}, bf16[144,75]{1,0:T(8,128)(2,1)S(1)}, u32[]{:S(2)}, u32[]{:S(2)}) collective-permute-start(bf16[144,75]{1,0:T(8,128)(2,1)S(1)} %copy-done), channel_id=1, source_target_pairs={{32,0},{36,4},{40,8},{44,12},{48,16},{52,20},{56,24},{60,28},{0,32... | collective-permute-start | bytes 64808 | tf_op jit(solution)/shard_map/ppermute | solution.py:315
  126.8 1.0 collective-permute-start.6
  127.8 5.5 %collective-permute-start.5 = (bf16[144,75]{1,0:T(8,128)(2,1)S(1)}, bf16[144,75]{1,0:T(8,128)(2,1)S(1)}, u32[]{:S(2)}, u32[]{:S(2)}) collective-permute-start(bf16[144,75]{1,0:T(8,128)(2,1)S(1)} %copy-done), channel_id=1, source_target_pairs={{24,0},{28,4},{32,8},{36,12},{40,16},{44,20},{48,24},{52,28},{56,3... | collective-permute-start | bytes 64808 | tf_op jit(solution)/shard_map/ppermute | solution.py:315
  133.3 1.4 collective-permute-start.4
  134.7 1.7 collective-permute-start.3
  136.3 2.6 %collective-permute-start.2 = (bf16[144,75]{1,0:T(8,128)(2,1)S(1)}, bf16[144,75]{1,0:T(8,128)(2,1)S(1)}, u32[]{:S(2)}, u32[]{:S(2)}) collective-permute-start(bf16[144,75]{1,0:T(8,128)(2,1)S(1)} %copy-done), channel_id=1, source_target_pairs={{12,0},{16,4},{20,8},{24,12},{28,16},{32,20},{36,24},{40,28},{44,3... | collective-permute-start | bytes 64808 | tf_op jit(solution)/shard_map/ppermute | solution.py:315
  138.9 2.7 %collective-permute-start = (bf16[144,75]{1,0:T(8,128)(2,1)S(1)}, bf16[144,75]{1,0:T(8,128)(2,1)S(1)}, u32[]{:S(2)}, u32[]{:S(2)}) collective-permute-start(bf16[144,75]{1,0:T(8,128)(2,1)S(1)} %copy-done), channel_id=1, source_target_pairs={{4,0},{8,4},{12,8},{16,12},{20,16},{24,20},{28,24},{32,28},{36,32}... | collective-permute-start | bytes 64808 | tf_op jit(solution)/shard_map/ppermute | solution.py:315
  141.7 2.2 fusion.14.sel
  144.0 0.4 collective-permute-done.1.refs_2_
  144.5 0.1 copy-done.11
  144.5 0.0 copy-done.12
  144.6 0.0 copy-done.13
  144.6 0.4 copy-done.14
  145.0 0.0 copy-done.15
  145.0 2.0 join.1
  147.0 1.2 copy.6
  148.2 0.3 pad.12
  148.5 0.9 copy.7
  149.3 0.1 pad.13
  149.4 1.0 reshape.29
  150.4 1.2 pad.14
  151.6 0.3 copy.12.cols
  151.8 0.3 copy.11.win
  152.1 11.6 %dress_first.1 = (bf16[2,1344,1344]{2,1,0:T(8,128)(2,1)}, bf16[4,384,1536]{2,1,0:T(8,128)(2,1)}) custom-call(bf16[64,112,256]{2,1,0:T(8,128)(2,1)} %all-to-all-done.1.pieces, bf16[256,1536]{1,0:T(8,128)(2,1)S(1)} %copy.11.win, bf16[256,1536]{1,0:T(8,128)(2,1)S(1)} %copy.12.cols, bf16[1536,256]{1,0:T(8,128)(2,1)S(1)} %fusion.14.sel), custom_call_target="tpu_custom_call" | custom-call | flops 10000000000 | bytes 10000000 | tf_op jit(solution)/shard_map/dress_first/pallas_call | solution.py:221
  163.7 13.2 %dress_last.1 = (bf16[2,1344,1344]{2,1,0:T(8,128)(2,1)}, bf16[32,112,256]{2,1,0:T(8,128)(2,1)S(1)}, bf16[32,112,256]{2,1,0:T(8,128)(2,1)S(1)}) custom-call(bf16[64,112,256]{2,1,0:T(8,128)(2,1)} %all-to-all-done.pieces, bf16[256,1536]{1,0:T(8,128)(2,1)S(1)} %copy.11.win, bf16[256,1536]{1,0:T(8,128)(2,1)S(1)} %copy.12.cols, ...), custom_call_target="tpu_custom_call", output_to_operand_aliasing={{0}: (6, {})} | custom-call | flops 10000000000 | bytes 10000000 | tf_op jit(solution)/shard_map/dress_last/pallas_call | solution.py:221
  176.9 0.1 collective-permute-start.15
  177.0 3.8 %collective-permute-done.15 = bf16[32,112,256]{2,1,0:T(8,128)(2,1)S(1)} collective-permute-done((bf16[32,112,256]{2,1,0:T(8,128)(2,1)S(1)}, bf16[32,112,256]{2,1,0:T(8,128)(2,1)S(1)}, u32[]{:S(2)}, u32[]{:S(2)}) %collective-permute-start.15) | collective-permute-done | bytes 1835040 | tf_op jit(solution)/shard_map/ppermute | solution.py:332
  180.7 0.5 add_convert_fusion
  181.3 37.1 %all_to_all.15 = bf16[32,112,256]{2,1,0:T(8,128)(2,1)S(1)} all-to-all(bf16[32,112,256]{2,1,0:T(8,128)(2,1)S(1)} %add_convert_fusion), channel_id=1, replica_groups=mesh['pb'=2,'row_0'=4,'row_1'=4,'col_0'=2,'col_1'=2] {'row_0','row_1','c..., dimensions={0} | all-to-all | bytes 3670016 | tf_op jit(solution)/shard_map/all_to_all | solution.py:306
  218.4 0.3 reduce_sum.12.own
  218.6 1.1 collective-permute-start.16
  219.7 3.2 %collective-permute-done.16.other = bf16[112,256]{1,0:T(8,128)(2,1)S(1)} collective-permute-done((bf16[112,256]{1,0:T(8,128)(2,1)S(1)}, bf16[112,256]{1,0:T(8,128)(2,1)S(1)}, u32[]{:S(2)}, u32[]{:S(2)}) %collective-permute-start.16) | collective-permute-done | bytes 57376 | tf_op jit(solution)/shard_map/ppermute | solution.py:336
  222.9 0.7 finish.1
  (46 shorter events, 0.1 us)
Async XLA Ops:
  8.3 58.3 %all-to-all-start.1 = ((bf16[64,112,256]{2,1,0:T(8,128)(2,1)}), bf16[64,112,256]{2,1,0:T(8,128)(2,1)}, u32[]{:S(2)}, u32[]{:S(2)}) async-start(bf16[64,112,256]{2,1,0:T(8,128)(2,1)} %pack.3), calls=%async_computation.1 | async-start | bytes 7340032 | tf_op jit(solution)/shard_map/all_to_all | solution.py:306
  27.7 46.8 %copy-start = (bf16[144,75]{1,0:T(8,128)(2,1)S(1)}, bf16[144,75]{1,0:T(8,128)(2,1)}, u32[]{:S(2)}) copy-start(bf16[144,75]{1,0:T(8,128)(2,1)} %refs_0_) | copy-start | bytes 64804
  66.6 97.1 %all-to-all-start = ((bf16[64,112,256]{2,1,0:T(8,128)(2,1)}), bf16[64,112,256]{2,1,0:T(8,128)(2,1)}, u32[]{:S(2)}, u32[]{:S(2)}) async-start(bf16[64,112,256]{2,1,0:T(8,128)(2,1)} %pack.2), calls=%async_computation | async-start | bytes 7340032 | tf_op jit(solution)/shard_map/all_to_all | solution.py:306
  74.5 46.4 %collective-permute-start.14 = (bf16[144,75]{1,0:T(8,128)(2,1)S(1)}, bf16[144,75]{1,0:T(8,128)(2,1)S(1)}, u32[]{:S(2)}, u32[]{:S(2)}) collective-permute-start(bf16[144,75]{1,0:T(8,128)(2,1)S(1)} %copy-done), channel_id=1, source_target_pairs={{60,0},{0,4},{4,8},{8,12},{12,16},{16,20},{20,24},{24,28},{28,32},... | collective-permute-start | bytes 64808 | tf_op jit(solution)/shard_map/ppermute | solution.py:315
  76.1 45.3 %collective-permute-start.13 = (bf16[144,75]{1,0:T(8,128)(2,1)S(1)}, bf16[144,75]{1,0:T(8,128)(2,1)S(1)}, u32[]{:S(2)}, u32[]{:S(2)}) collective-permute-start(bf16[144,75]{1,0:T(8,128)(2,1)S(1)} %copy-done), channel_id=1, source_target_pairs={{56,0},{60,4},{0,8},{4,12},{8,16},{12,20},{16,24},{20,28},{24,32},... | collective-permute-start | bytes 64808 | tf_op jit(solution)/shard_map/ppermute | solution.py:315
  78.8 44.1 %collective-permute-start.12 = (bf16[144,75]{1,0:T(8,128)(2,1)S(1)}, bf16[144,75]{1,0:T(8,128)(2,1)S(1)}, u32[]{:S(2)}, u32[]{:S(2)}) collective-permute-start(bf16[144,75]{1,0:T(8,128)(2,1)S(1)} %copy-done), channel_id=1, source_target_pairs={{52,0},{56,4},{60,8},{0,12},{4,16},{8,20},{12,24},{16,28},{20,32},... | collective-permute-start | bytes 64808 | tf_op jit(solution)/shard_map/ppermute | solution.py:315
  81.2 45.6 %collective-permute-start.11 = (bf16[144,75]{1,0:T(8,128)(2,1)S(1)}, bf16[144,75]{1,0:T(8,128)(2,1)S(1)}, u32[]{:S(2)}, u32[]{:S(2)}) collective-permute-start(bf16[144,75]{1,0:T(8,128)(2,1)S(1)} %copy-done), channel_id=1, source_target_pairs={{48,0},{52,4},{56,8},{60,12},{0,16},{4,20},{8,24},{12,28},{16,32},... | collective-permute-start | bytes 64808 | tf_op jit(solution)/shard_map/ppermute | solution.py:315
  82.7 45.0 %collective-permute-start.10 = (bf16[144,75]{1,0:T(8,128)(2,1)S(1)}, bf16[144,75]{1,0:T(8,128)(2,1)S(1)}, u32[]{:S(2)}, u32[]{:S(2)}) collective-permute-start(bf16[144,75]{1,0:T(8,128)(2,1)S(1)} %copy-done), channel_id=1, source_target_pairs={{44,0},{48,4},{52,8},{56,12},{60,16},{0,20},{4,24},{8,28},{12,32},... | collective-permute-start | bytes 64808 | tf_op jit(solution)/shard_map/ppermute | solution.py:315
  120.9 23.5 %copy-start.1 = (bf16[144,75]{1,0:T(8,128)(2,1)}, bf16[144,75]{1,0:T(8,128)(2,1)S(1)}, u32[]{:S(2)}) copy-start(bf16[144,75]{1,0:T(8,128)(2,1)S(1)} %collective-permute-done.14.refs_15_) | copy-start | bytes 64804
  120.9 12.3 %collective-permute-start.9 = (bf16[144,75]{1,0:T(8,128)(2,1)S(1)}, bf16[144,75]{1,0:T(8,128)(2,1)S(1)}, u32[]{:S(2)}, u32[]{:S(2)}) collective-permute-start(bf16[144,75]{1,0:T(8,128)(2,1)S(1)} %copy-done), channel_id=1, source_target_pairs={{40,0},{44,4},{48,8},{52,12},{56,16},{60,20},{0,24},{4,28},{8,32},... | collective-permute-start | bytes 64808 | tf_op jit(solution)/shard_map/ppermute | solution.py:315
  121.4 23.0 %copy-start.2 = (bf16[144,75]{1,0:T(8,128)(2,1)}, bf16[144,75]{1,0:T(8,128)(2,1)S(1)}, u32[]{:S(2)}) copy-start(bf16[144,75]{1,0:T(8,128)(2,1)S(1)} %collective-permute-done.13.refs_14_) | copy-start | bytes 64804
  121.4 13.3 %collective-permute-start.8 = (bf16[144,75]{1,0:T(8,128)(2,1)S(1)}, bf16[144,75]{1,0:T(8,128)(2,1)S(1)}, u32[]{:S(2)}, u32[]{:S(2)}) collective-permute-start(bf16[144,75]{1,0:T(8,128)(2,1)S(1)} %copy-done), channel_id=1, source_target_pairs={{36,0},{40,4},{44,8},{48,12},{52,16},{56,20},{60,24},{0,28},{4,32}... | collective-permute-start | bytes 64808 | tf_op jit(solution)/shard_map/ppermute | solution.py:315
  122.8 21.6 %copy-start.3 = (bf16[144,75]{1,0:T(8,128)(2,1)}, bf16[144,75]{1,0:T(8,128)(2,1)S(1)}, u32[]{:S(2)}) copy-start(bf16[144,75]{1,0:T(8,128)(2,1)S(1)} %collective-permute-done.12.refs_13_) | copy-start | bytes 64804
  122.8 13.5 %collective-permute-start.7 = (bf16[144,75]{1,0:T(8,128)(2,1)S(1)}, bf16[144,75]{1,0:T(8,128)(2,1)S(1)}, u32[]{:S(2)}, u32[]{:S(2)}) collective-permute-start(bf16[144,75]{1,0:T(8,128)(2,1)S(1)} %copy-done), channel_id=1, source_target_pairs={{32,0},{36,4},{40,8},{44,12},{48,16},{52,20},{56,24},{60,28},{0,32... | collective-permute-start | bytes 64808 | tf_op jit(solution)/shard_map/ppermute | solution.py:315
  126.8 17.6 %copy-start.4 = (bf16[144,75]{1,0:T(8,128)(2,1)}, bf16[144,75]{1,0:T(8,128)(2,1)S(1)}, u32[]{:S(2)}) copy-start(bf16[144,75]{1,0:T(8,128)(2,1)S(1)} %collective-permute-done.11.refs_12_) | copy-start | bytes 64804
  126.8 12.1 %collective-permute-start.6 = (bf16[144,75]{1,0:T(8,128)(2,1)S(1)}, bf16[144,75]{1,0:T(8,128)(2,1)S(1)}, u32[]{:S(2)}, u32[]{:S(2)}) collective-permute-start(bf16[144,75]{1,0:T(8,128)(2,1)S(1)} %copy-done), channel_id=1, source_target_pairs={{28,0},{32,4},{36,8},{40,12},{44,16},{48,20},{52,24},{56,28},{60,3... | collective-permute-start | bytes 64808 | tf_op jit(solution)/shard_map/ppermute | solution.py:315
  127.8 16.7 %copy-start.5 = (bf16[144,75]{1,0:T(8,128)(2,1)}, bf16[144,75]{1,0:T(8,128)(2,1)S(1)}, u32[]{:S(2)}) copy-start(bf16[144,75]{1,0:T(8,128)(2,1)S(1)} %collective-permute-done.10.refs_11_) | copy-start | bytes 64804
  127.8 11.2 %collective-permute-start.5 = (bf16[144,75]{1,0:T(8,128)(2,1)S(1)}, bf16[144,75]{1,0:T(8,128)(2,1)S(1)}, u32[]{:S(2)}, u32[]{:S(2)}) collective-permute-start(bf16[144,75]{1,0:T(8,128)(2,1)S(1)} %copy-done), channel_id=1, source_target_pairs={{24,0},{28,4},{32,8},{36,12},{40,16},{44,20},{48,24},{52,28},{56,3... | collective-permute-start | bytes 64808 | tf_op jit(solution)/shard_map/ppermute | solution.py:315
  133.3 11.2 %copy-start.6 = (bf16[144,75]{1,0:T(8,128)(2,1)}, bf16[144,75]{1,0:T(8,128)(2,1)S(1)}, u32[]{:S(2)}) copy-start(bf16[144,75]{1,0:T(8,128)(2,1)S(1)} %collective-permute-done.9.refs_10_) | copy-start | bytes 64804
  133.3 10.6 %collective-permute-start.4 = (bf16[144,75]{1,0:T(8,128)(2,1)S(1)}, bf16[144,75]{1,0:T(8,128)(2,1)S(1)}, u32[]{:S(2)}, u32[]{:S(2)}) collective-permute-start(bf16[144,75]{1,0:T(8,128)(2,1)S(1)} %copy-done), channel_id=1, source_target_pairs={{20,0},{24,4},{28,8},{32,12},{36,16},{40,20},{44,24},{48,28},{52,3... | collective-permute-start | bytes 64808 | tf_op jit(solution)/shard_map/ppermute | solution.py:315
  134.6 9.8 %copy-start.7 = (bf16[144,75]{1,0:T(8,128)(2,1)}, bf16[144,75]{1,0:T(8,128)(2,1)S(1)}, u32[]{:S(2)}) copy-start(bf16[144,75]{1,0:T(8,128)(2,1)S(1)} %collective-permute-done.8.refs_9_) | copy-start | bytes 64804
  134.7 9.3 %collective-permute-start.3 = (bf16[144,75]{1,0:T(8,128)(2,1)S(1)}, bf16[144,75]{1,0:T(8,128)(2,1)S(1)}, u32[]{:S(2)}, u32[]{:S(2)}) collective-permute-start(bf16[144,75]{1,0:T(8,128)(2,1)S(1)} %copy-done), channel_id=1, source_target_pairs={{16,0},{20,4},{24,8},{28,12},{32,16},{36,20},{40,24},{44,28},{48,3... | collective-permute-start | bytes 64808 | tf_op jit(solution)/shard_map/ppermute | solution.py:315
  136.3 8.1 %copy-start.8 = (bf16[144,75]{1,0:T(8,128)(2,1)}, bf16[144,75]{1,0:T(8,128)(2,1)S(1)}, u32[]{:S(2)}) copy-start(bf16[144,75]{1,0:T(8,128)(2,1)S(1)} %collective-permute-done.7.refs_8_) | copy-start | bytes 64804
  136.3 7.7 %collective-permute-start.2 = (bf16[144,75]{1,0:T(8,128)(2,1)S(1)}, bf16[144,75]{1,0:T(8,128)(2,1)S(1)}, u32[]{:S(2)}, u32[]{:S(2)}) collective-permute-start(bf16[144,75]{1,0:T(8,128)(2,1)S(1)} %copy-done), channel_id=1, source_target_pairs={{12,0},{16,4},{20,8},{24,12},{28,16},{32,20},{36,24},{40,28},{44,3... | collective-permute-start | bytes 64808 | tf_op jit(solution)/shard_map/ppermute | solution.py:315
  138.9 5.6 %copy-start.9 = (bf16[144,75]{1,0:T(8,128)(2,1)}, bf16[144,75]{1,0:T(8,128)(2,1)S(1)}, u32[]{:S(2)}) copy-start(bf16[144,75]{1,0:T(8,128)(2,1)S(1)} %collective-permute-done.6.refs_7_) | copy-start | bytes 64804
  138.9 5.5 %collective-permute-start.1 = (bf16[144,75]{1,0:T(8,128)(2,1)S(1)}, bf16[144,75]{1,0:T(8,128)(2,1)S(1)}, u32[]{:S(2)}, u32[]{:S(2)}) collective-permute-start(bf16[144,75]{1,0:T(8,128)(2,1)S(1)} %copy-done), channel_id=1, source_target_pairs={{8,0},{12,4},{16,8},{20,12},{24,16},{28,20},{32,24},{36,28},{40,32... | collective-permute-start | bytes 64808 | tf_op jit(solution)/shard_map/ppermute | solution.py:315
  138.9 5.5 %copy-start.10 = (bf16[144,75]{1,0:T(8,128)(2,1)}, bf16[144,75]{1,0:T(8,128)(2,1)S(1)}, u32[]{:S(2)}) copy-start(bf16[144,75]{1,0:T(8,128)(2,1)S(1)} %collective-permute-done.5.refs_6_) | copy-start | bytes 64804
  138.9 5.4 %collective-permute-start = (bf16[144,75]{1,0:T(8,128)(2,1)S(1)}, bf16[144,75]{1,0:T(8,128)(2,1)S(1)}, u32[]{:S(2)}, u32[]{:S(2)}) collective-permute-start(bf16[144,75]{1,0:T(8,128)(2,1)S(1)} %copy-done), channel_id=1, source_target_pairs={{4,0},{8,4},{12,8},{16,12},{20,16},{24,20},{28,24},{32,28},{36,32}... | collective-permute-start | bytes 64808 | tf_op jit(solution)/shard_map/ppermute | solution.py:315
  143.9 0.6 copy-start.11
  144.0 0.6 copy-start.12
  144.0 0.6 copy-start.13
  144.4 0.6 copy-start.14
  144.4 0.6 copy-start.15
  176.9 3.9 %collective-permute-start.15 = (bf16[32,112,256]{2,1,0:T(8,128)(2,1)S(1)}, bf16[32,112,256]{2,1,0:T(8,128)(2,1)S(1)}, u32[]{:S(2)}, u32[]{:S(2)}) collective-permute-start(bf16[32,112,256]{2,1,0:T(8,128)(2,1)S(1)} %get-tuple-element.15), channel_id=1, source_target_pairs={{0,1},{1,0},{2,3},{3,2},{4,5},{5,4},{6,7},{7,6},{8,9},{9,8},{10,11... | collective-permute-start | bytes 5505032 | tf_op jit(solution)/shard_map/ppermute | solution.py:332
  218.6 4.3 %collective-permute-start.16 = (bf16[112,256]{1,0:T(8,128)(2,1)S(1)}, bf16[112,256]{1,0:T(8,128)(2,1)S(1)}, u32[]{:S(2)}, u32[]{:S(2)}) collective-permute-start(bf16[112,256]{1,0:T(8,128)(2,1)S(1)} %reduce_sum.12.own), channel_id=1, source_target_pairs={{0,64},{64,0},{1,65},{65,1},{2,66},{66,2},{3,67},{67,3},{4,68},{68... | collective-permute-start | bytes 172040 | tf_op jit(solution)/shard_map/ppermute | solution.py:336

commit v5 on v4

--- a/solution.py
+++ b/solution.py
@@ -264,16 +264,36 @@
     )(own, other)
 
 
+def fold(amp, out):
+    tall, wide = out.shape[0], amp.shape[1]
+    out[...] = jnp.zeros_like(out)
+    for i in range(amp.shape[0] // tall):
+        out[:, i * FULL : i * FULL + wide] = amp[i * tall : (i + 1) * tall, :]
+
+
+def fold_call(amp):
+    return pl.pallas_call(
+        fold,
+        out_shape=jax.ShapeDtypeStruct((amp.shape[0] // 3, LANES), amp.dtype),
+        in_specs=[VMEM],
+        out_specs=VMEM,
+        name="fold",
+    )(amp)
+
+
 def join(here, *refs):
-    count = len(refs) - 1
+    count, out = len(refs) - 1, refs[-1]
+    tall, wide = refs[0].shape[0], out.shape[2]
     for step in range(count):
-        refs[-1][lax.rem(here[0] + step, count)] = refs[step][...]
-
-
-def join_call(here, parts):
+        to = lax.rem(here[0] + step, count)
+        for i in range(out.shape[1] // tall):
+            out[to, i * tall : (i + 1) * tall, :] = refs[step][:, i * FULL : i * FULL + wide]
+
+
+def join_call(here, parts, shape):
     return pl.pallas_call(
         join,
-        out_shape=jax.ShapeDtypeStruct((len(parts), *parts[0].shape), parts[0].dtype),
+        out_shape=jax.ShapeDtypeStruct((len(parts), *shape), parts[0].dtype),
         in_specs=[pl.BlockSpec(memory_space=pltpu.SMEM)] + [VMEM] * len(parts),
         out_specs=VMEM,
         name="join",
@@ -309,11 +329,12 @@
 def all_of(array, axis):
     count = lax.axis_size(axis)
     here = lax.axis_index(axis)
-    found = [array]
+    folded = fold_call(array)
+    found = [folded]
     for step in range(1, count):
         pairs = [((to + step) % count, to) for to in range(count)]
-        found.append(lax.ppermute(array, axis, pairs))
-    return join_call(here.astype(jnp.int32).reshape(1), found)
+        found.append(lax.ppermute(folded, axis, pairs))
+    return join_call(here.astype(jnp.int32).reshape(1), found, array.shape)
 
 
 def step(chol, amplitudes):

time: 224 us -> 224 us (level)
  transfers between devices with their start and end apart: 19 -> 19, of which waited for: 5 -> 6; matrix products, arithmetic and copies ran while one was open for 3% -> 3% of each run, Pallas kernels for 9% -> 10%
where the time goes in v5:
time: 224 us; the launch traced here: 223 us
  waiting for transfers between devices  81.4 us (36%)
  starting transfers between devices  50.4 us (22%)
  Pallas kernels  44.3 us (20%)
  blocking collectives  37.2 us (17%)
  local copies, waits for them, and re-layouts  5.63 us (3%)
  other arithmetic  3.07 us (1%)
    all_to_all x2, waiting for transfers between devices, swap(): return lax.all_to_all(array, axis, split_axis=0, concat_axis=0, tiled=True)  38.9 us
    all_to_all x1, blocking collectives, swap(): return lax.all_to_all(array, axis, split_axis=0, concat_axis=0, tiled=True)  37.2 us
    ppermute x15, waiting for transfers between devices, all_of(): found.append(lax.ppermute(folded, axis, pairs))  35.6 us
    ppermute x15, starting transfers between devices, all_of(): found.append(lax.ppermute(folded, axis, pairs))  29.7 us
    pallas_call x2, Pallas kernels, dress_call(): pl.pallas_call(functools.partial(dress, own, last), out_shape=out_shape,...  24.7 us
    all_to_all x2, starting transfers between devices, swap(): return lax.all_to_all(array, axis, split_axis=0, concat_axis=0, tiled=True)  19.5 us
    pallas_call x2, Pallas kernels, pack_call(): pl.pallas_call(functools.partial(pack, own, q_own), out_shape=pltpu.HBM((...  15.4 us
  transfers between devices with their start and end apart: 19, of which 6 were waited for; matrix products, arithmetic and copies ran while one was open for 3% of the time, Pallas kernels for 10%

profile of v5, /device:TPU:0, one launch (start us, length us, event | category | flops | bytes accessed | tf_op | source)
XLA Modules:
  0.0 223.0 jit_solution(16927643680303706621)
XLA Ops:
  0.6 7.7 %pack.3 = bf16[64,112,256]{2,1,0:T(8,128)(2,1)} custom-call(bf16[84,336,128]{2,1,0:T(8,128)(2,1)} %bitcast.17), custom_call_target="tpu_custom_call" | custom-call | flops 5000000000 | bytes 10000000 | tf_op jit(solution)/shard_map/pack/pallas_call | solution.py:75
  8.3 11.6 %all-to-all-start.1 = ((bf16[64,112,256]{2,1,0:T(8,128)(2,1)}), bf16[64,112,256]{2,1,0:T(8,128)(2,1)}, u32[]{:S(2)}, u32[]{:S(2)}) async-start(bf16[64,112,256]{2,1,0:T(8,128)(2,1)} %pack.3), calls=%async_computation.1 | async-start | bytes 7340032 | tf_op jit(solution)/shard_map/all_to_all | solution.py:326
  19.9 7.7 %pack.2 = bf16[64,112,256]{2,1,0:T(8,128)(2,1)} custom-call(bf16[84,336,128]{2,1,0:T(8,128)(2,1)} %bitcast.18), custom_call_target="tpu_custom_call" | custom-call | flops 5000000000 | bytes 10000000 | tf_op jit(solution)/shard_map/pack/pallas_call | solution.py:75
  27.7 38.9 %all-to-all-done.1.pieces = bf16[64,112,256]{2,1,0:T(8,128)(2,1)} async-done(((bf16[64,112,256]{2,1,0:T(8,128)(2,1)}), bf16[64,112,256]{2,1,0:T(8,128)(2,1)}, u32[]{:S(2)}, u32[]{:S(2)}) %all-to-all-start.1) | async-done | bytes 3670048 | tf_op jit(solution)/shard_map/all_to_all | solution.py:326
  66.6 7.9 %all-to-all-start = ((bf16[64,112,256]{2,1,0:T(8,128)(2,1)}), bf16[64,112,256]{2,1,0:T(8,128)(2,1)}, u32[]{:S(2)}, u32[]{:S(2)}) async-start(bf16[64,112,256]{2,1,0:T(8,128)(2,1)} %pack.2), calls=%async_computation | async-start | bytes 7340032 | tf_op jit(solution)/shard_map/all_to_all | solution.py:326
  74.5 1.5 fold.1.refs_0_
  76.0 1.5 collective-permute-start.14
  77.5 2.7 %collective-permute-start.13 = (bf16[48,256]{1,0:T(8,128)(2,1)}, bf16[48,256]{1,0:T(8,128)(2,1)S(1)}, u32[]{:S(2)}, u32[]{:S(2)}) collective-permute-start(bf16[48,256]{1,0:T(8,128)(2,1)} %fold.1.refs_0_), channel_id=1, source_target_pairs={{56,0},{60,4},{0,8},{4,12},{8,16},{12,20},{16,24},{20,28},{24,32},... | collective-permute-start | bytes 73736 | tf_op jit(solution)/shard_map/ppermute | solution.py:336
  80.1 2.4 %collective-permute-start.12 = (bf16[48,256]{1,0:T(8,128)(2,1)}, bf16[48,256]{1,0:T(8,128)(2,1)S(1)}, u32[]{:S(2)}, u32[]{:S(2)}) collective-permute-start(bf16[48,256]{1,0:T(8,128)(2,1)} %fold.1.refs_0_), channel_id=1, source_target_pairs={{52,0},{56,4},{60,8},{0,12},{4,16},{8,20},{12,24},{16,28},{20,32},... | collective-permute-start | bytes 73736 | tf_op jit(solution)/shard_map/ppermute | solution.py:336
  82.5 1.6 collective-permute-start.11
  84.1 1.3 collective-permute-start.10
  85.5 35.0 %collective-permute-done.14.refs_15_ = bf16[48,256]{1,0:T(8,128)(2,1)S(1)} collective-permute-done((bf16[48,256]{1,0:T(8,128)(2,1)}, bf16[48,256]{1,0:T(8,128)(2,1)S(1)}, u32[]{:S(2)}, u32[]{:S(2)}) %collective-permute-start.14) | collective-permute-done | bytes 24608 | tf_op jit(solution)/shard_map/ppermute | solution.py:336
  120.5 0.2 collective-permute-start.9
  120.7 0.1 collective-permute-done.13.refs_14_
  120.8 1.8 collective-permute-start.8
  122.6 0.0 collective-permute-done.12.refs_13_
  122.6 3.6 %collective-permute-start.7 = (bf16[48,256]{1,0:T(8,128)(2,1)}, bf16[48,256]{1,0:T(8,128)(2,1)S(1)}, u32[]{:S(2)}, u32[]{:S(2)}) collective-permute-start(bf16[48,256]{1,0:T(8,128)(2,1)} %fold.1.refs_0_), channel_id=1, source_target_pairs={{32,0},{36,4},{40,8},{44,12},{48,16},{52,20},{56,24},{60,28},{0,32... | collective-permute-start | bytes 73736 | tf_op jit(solution)/shard_map/ppermute | solution.py:336
  126.1 1.1 collective-permute-start.6
  127.2 0.0 collective-permute-done.10.refs_11_
  127.2 5.6 %collective-permute-start.5 = (bf16[48,256]{1,0:T(8,128)(2,1)}, bf16[48,256]{1,0:T(8,128)(2,1)S(1)}, u32[]{:S(2)}, u32[]{:S(2)}) collective-permute-start(bf16[48,256]{1,0:T(8,128)(2,1)} %fold.1.refs_0_), channel_id=1, source_target_pairs={{24,0},{28,4},{32,8},{36,12},{40,16},{44,20},{48,24},{52,28},{56,3... | collective-permute-start | bytes 73736 | tf_op jit(solution)/shard_map/ppermute | solution.py:336
  132.8 1.0 collective-permute-start.4
  133.8 1.8 collective-permute-start.3
  135.6 2.5 %collective-permute-start.2 = (bf16[48,256]{1,0:T(8,128)(2,1)}, bf16[48,256]{1,0:T(8,128)(2,1)S(1)}, u32[]{:S(2)}, u32[]{:S(2)}) collective-permute-start(bf16[48,256]{1,0:T(8,128)(2,1)} %fold.1.refs_0_), channel_id=1, source_target_pairs={{12,0},{16,4},{20,8},{24,12},{28,16},{32,20},{36,24},{40,28},{44,3... | collective-permute-start | bytes 73736 | tf_op jit(solution)/shard_map/ppermute | solution.py:336
  138.1 0.0 collective-permute-done.6.refs_7_
  138.2 2.7 %collective-permute-start = (bf16[48,256]{1,0:T(8,128)(2,1)}, bf16[48,256]{1,0:T(8,128)(2,1)S(1)}, u32[]{:S(2)}, u32[]{:S(2)}) collective-permute-start(bf16[48,256]{1,0:T(8,128)(2,1)} %fold.1.refs_0_), channel_id=1, source_target_pairs={{4,0},{8,4},{12,8},{16,12},{20,16},{24,20},{28,24},{32,28},{36,32}... | collective-permute-start | bytes 73736 | tf_op jit(solution)/shard_map/ppermute | solution.py:336
  140.9 2.2 fusion.14.sel
  143.2 0.5 collective-permute-done.1.refs_2_
  143.8 0.5 copy-done.13
  144.3 0.0 copy-done.14
  144.3 2.0 join.1
  146.3 1.2 copy.6
  147.5 0.3 pad.12
  147.8 0.9 copy.7
  148.7 0.1 pad.13
  148.8 1.0 reshape.29
  149.7 1.2 pad.14
  150.9 0.3 copy.12.cols
  151.2 0.3 copy.11.win
  151.5 11.5 %dress_first.1 = (bf16[2,1344,1344]{2,1,0:T(8,128)(2,1)}, bf16[4,384,1536]{2,1,0:T(8,128)(2,1)}) custom-call(bf16[64,112,256]{2,1,0:T(8,128)(2,1)} %all-to-all-done.1.pieces, bf16[256,1536]{1,0:T(8,128)(2,1)S(1)} %copy.11.win, bf16[256,1536]{1,0:T(8,128)(2,1)S(1)} %copy.12.cols, bf16[1536,256]{1,0:T(8,128)(2,1)S(1)} %fusion.14.sel), custom_call_target="tpu_custom_call" | custom-call | flops 10000000000 | bytes 10000000 | tf_op jit(solution)/shard_map/dress_first/pallas_call | solution.py:221
  163.0 13.2 %dress_last.1 = (bf16[2,1344,1344]{2,1,0:T(8,128)(2,1)}, bf16[32,112,256]{2,1,0:T(8,128)(2,1)S(1)}, bf16[32,112,256]{2,1,0:T(8,128)(2,1)S(1)}) custom-call(bf16[64,112,256]{2,1,0:T(8,128)(2,1)} %all-to-all-done.pieces, bf16[256,1536]{1,0:T(8,128)(2,1)S(1)} %copy.11.win, bf16[256,1536]{1,0:T(8,128)(2,1)S(1)} %copy.12.cols, ...), custom_call_target="tpu_custom_call", output_to_operand_aliasing={{0}: (6, {})} | custom-call | flops 10000000000 | bytes 10000000 | tf_op jit(solution)/shard_map/dress_last/pallas_call | solution.py:221
  176.2 0.1 collective-permute-start.15
  176.3 3.8 %collective-permute-done.15 = bf16[32,112,256]{2,1,0:T(8,128)(2,1)S(1)} collective-permute-done((bf16[32,112,256]{2,1,0:T(8,128)(2,1)S(1)}, bf16[32,112,256]{2,1,0:T(8,128)(2,1)S(1)}, u32[]{:S(2)}, u32[]{:S(2)}) %collective-permute-start.15) | collective-permute-done | bytes 1835040 | tf_op jit(solution)/shard_map/ppermute | solution.py:353
  180.1 0.5 add_convert_fusion
  180.6 37.2 %all_to_all.15 = bf16[32,112,256]{2,1,0:T(8,128)(2,1)S(1)} all-to-all(bf16[32,112,256]{2,1,0:T(8,128)(2,1)S(1)} %add_convert_fusion), channel_id=1, replica_groups=mesh['pb'=2,'row_0'=4,'row_1'=4,'col_0'=2,'col_1'=2] {'row_0','row_1','c..., dimensions={0} | all-to-all | bytes 3670016 | tf_op jit(solution)/shard_map/all_to_all | solution.py:326
  217.8 0.3 reduce_sum.12.own
  218.0 1.1 collective-permute-start.16
  219.1 3.2 %collective-permute-done.16.other = bf16[112,256]{1,0:T(8,128)(2,1)S(1)} collective-permute-done((bf16[112,256]{1,0:T(8,128)(2,1)S(1)}, bf16[112,256]{1,0:T(8,128)(2,1)S(1)}, u32[]{:S(2)}, u32[]{:S(2)}) %collective-permute-start.16) | collective-permute-done | bytes 57376 | tf_op jit(solution)/shard_map/ppermute | solution.py:357
  222.3 0.7 finish.1
  (45 shorter events, 0.1 us)
Async XLA Ops:
  8.3 58.3 %all-to-all-start.1 = ((bf16[64,112,256]{2,1,0:T(8,128)(2,1)}), bf16[64,112,256]{2,1,0:T(8,128)(2,1)}, u32[]{:S(2)}, u32[]{:S(2)}) async-start(bf16[64,112,256]{2,1,0:T(8,128)(2,1)} %pack.3), calls=%async_computation.1 | async-start | bytes 7340032 | tf_op jit(solution)/shard_map/all_to_all | solution.py:326
  66.6 96.4 %all-to-all-start = ((bf16[64,112,256]{2,1,0:T(8,128)(2,1)}), bf16[64,112,256]{2,1,0:T(8,128)(2,1)}, u32[]{:S(2)}, u32[]{:S(2)}) async-start(bf16[64,112,256]{2,1,0:T(8,128)(2,1)} %pack.2), calls=%async_computation | async-start | bytes 7340032 | tf_op jit(solution)/shard_map/all_to_all | solution.py:326
  76.0 44.5 %collective-permute-start.14 = (bf16[48,256]{1,0:T(8,128)(2,1)}, bf16[48,256]{1,0:T(8,128)(2,1)S(1)}, u32[]{:S(2)}, u32[]{:S(2)}) collective-permute-start(bf16[48,256]{1,0:T(8,128)(2,1)} %fold.1.refs_0_), channel_id=1, source_target_pairs={{60,0},{0,4},{4,8},{8,12},{12,16},{16,20},{20,24},{24,28},{28,32},... | collective-permute-start | bytes 73736 | tf_op jit(solution)/shard_map/ppermute | solution.py:336
  77.5 43.3 %collective-permute-start.13 = (bf16[48,256]{1,0:T(8,128)(2,1)}, bf16[48,256]{1,0:T(8,128)(2,1)S(1)}, u32[]{:S(2)}, u32[]{:S(2)}) collective-permute-start(bf16[48,256]{1,0:T(8,128)(2,1)} %fold.1.refs_0_), channel_id=1, source_target_pairs={{56,0},{60,4},{0,8},{4,12},{8,16},{12,20},{16,24},{20,28},{24,32},... | collective-permute-start | bytes 73736 | tf_op jit(solution)/shard_map/ppermute | solution.py:336
  80.1 42.4 %collective-permute-start.12 = (bf16[48,256]{1,0:T(8,128)(2,1)}, bf16[48,256]{1,0:T(8,128)(2,1)S(1)}, u32[]{:S(2)}, u32[]{:S(2)}) collective-permute-start(bf16[48,256]{1,0:T(8,128)(2,1)} %fold.1.refs_0_), channel_id=1, source_target_pairs={{52,0},{56,4},{60,8},{0,12},{4,16},{8,20},{12,24},{16,28},{20,32},... | collective-permute-start | bytes 73736 | tf_op jit(solution)/shard_map/ppermute | solution.py:336
  82.5 43.6 %collective-permute-start.11 = (bf16[48,256]{1,0:T(8,128)(2,1)}, bf16[48,256]{1,0:T(8,128)(2,1)S(1)}, u32[]{:S(2)}, u32[]{:S(2)}) collective-permute-start(bf16[48,256]{1,0:T(8,128)(2,1)} %fold.1.refs_0_), channel_id=1, source_target_pairs={{48,0},{52,4},{56,8},{60,12},{0,16},{4,20},{8,24},{12,28},{16,32},... | collective-permute-start | bytes 73736 | tf_op jit(solution)/shard_map/ppermute | solution.py:336
  84.1 43.1 %collective-permute-start.10 = (bf16[48,256]{1,0:T(8,128)(2,1)}, bf16[48,256]{1,0:T(8,128)(2,1)S(1)}, u32[]{:S(2)}, u32[]{:S(2)}) collective-permute-start(bf16[48,256]{1,0:T(8,128)(2,1)} %fold.1.refs_0_), channel_id=1, source_target_pairs={{44,0},{48,4},{52,8},{56,12},{60,16},{0,20},{4,24},{8,28},{12,32},... | collective-permute-start | bytes 73736 | tf_op jit(solution)/shard_map/ppermute | solution.py:336
  120.4 23.2 %copy-start = (bf16[48,256]{1,0:T(8,128)(2,1)}, bf16[48,256]{1,0:T(8,128)(2,1)S(1)}, u32[]{:S(2)}) copy-start(bf16[48,256]{1,0:T(8,128)(2,1)S(1)} %collective-permute-done.14.refs_15_) | copy-start | bytes 73732
  120.5 12.4 %collective-permute-start.9 = (bf16[48,256]{1,0:T(8,128)(2,1)}, bf16[48,256]{1,0:T(8,128)(2,1)S(1)}, u32[]{:S(2)}, u32[]{:S(2)}) collective-permute-start(bf16[48,256]{1,0:T(8,128)(2,1)} %fold.1.refs_0_), channel_id=1, source_target_pairs={{40,0},{44,4},{48,8},{52,12},{56,16},{60,20},{0,24},{4,28},{8,32},... | collective-permute-start | bytes 73736 | tf_op jit(solution)/shard_map/ppermute | solution.py:336
  120.8 22.9 %copy-start.1 = (bf16[48,256]{1,0:T(8,128)(2,1)}, bf16[48,256]{1,0:T(8,128)(2,1)S(1)}, u32[]{:S(2)}) copy-start(bf16[48,256]{1,0:T(8,128)(2,1)S(1)} %collective-permute-done.13.refs_14_) | copy-start | bytes 73732
  120.8 13.0 %collective-permute-start.8 = (bf16[48,256]{1,0:T(8,128)(2,1)}, bf16[48,256]{1,0:T(8,128)(2,1)S(1)}, u32[]{:S(2)}, u32[]{:S(2)}) collective-permute-start(bf16[48,256]{1,0:T(8,128)(2,1)} %fold.1.refs_0_), channel_id=1, source_target_pairs={{36,0},{40,4},{44,8},{48,12},{52,16},{56,20},{60,24},{0,28},{4,32}... | collective-permute-start | bytes 73736 | tf_op jit(solution)/shard_map/ppermute | solution.py:336
  122.6 21.1 %copy-start.2 = (bf16[48,256]{1,0:T(8,128)(2,1)}, bf16[48,256]{1,0:T(8,128)(2,1)S(1)}, u32[]{:S(2)}) copy-start(bf16[48,256]{1,0:T(8,128)(2,1)S(1)} %collective-permute-done.12.refs_13_) | copy-start | bytes 73732
  122.6 13.0 %collective-permute-start.7 = (bf16[48,256]{1,0:T(8,128)(2,1)}, bf16[48,256]{1,0:T(8,128)(2,1)S(1)}, u32[]{:S(2)}, u32[]{:S(2)}) collective-permute-start(bf16[48,256]{1,0:T(8,128)(2,1)} %fold.1.refs_0_), channel_id=1, source_target_pairs={{32,0},{36,4},{40,8},{44,12},{48,16},{52,20},{56,24},{60,28},{0,32... | collective-permute-start | bytes 73736 | tf_op jit(solution)/shard_map/ppermute | solution.py:336
  126.1 17.6 %copy-start.3 = (bf16[48,256]{1,0:T(8,128)(2,1)}, bf16[48,256]{1,0:T(8,128)(2,1)S(1)}, u32[]{:S(2)}) copy-start(bf16[48,256]{1,0:T(8,128)(2,1)S(1)} %collective-permute-done.11.refs_12_) | copy-start | bytes 73732
  126.1 12.0 %collective-permute-start.6 = (bf16[48,256]{1,0:T(8,128)(2,1)}, bf16[48,256]{1,0:T(8,128)(2,1)S(1)}, u32[]{:S(2)}, u32[]{:S(2)}) collective-permute-start(bf16[48,256]{1,0:T(8,128)(2,1)} %fold.1.refs_0_), channel_id=1, source_target_pairs={{28,0},{32,4},{36,8},{40,12},{44,16},{48,20},{52,24},{56,28},{60,3... | collective-permute-start | bytes 73736 | tf_op jit(solution)/shard_map/ppermute | solution.py:336
  127.2 16.5 %copy-start.4 = (bf16[48,256]{1,0:T(8,128)(2,1)}, bf16[48,256]{1,0:T(8,128)(2,1)S(1)}, u32[]{:S(2)}) copy-start(bf16[48,256]{1,0:T(8,128)(2,1)S(1)} %collective-permute-done.10.refs_11_) | copy-start | bytes 73732
  127.2 10.9 %collective-permute-start.5 = (bf16[48,256]{1,0:T(8,128)(2,1)}, bf16[48,256]{1,0:T(8,128)(2,1)S(1)}, u32[]{:S(2)}, u32[]{:S(2)}) collective-permute-start(bf16[48,256]{1,0:T(8,128)(2,1)} %fold.1.refs_0_), channel_id=1, source_target_pairs={{24,0},{28,4},{32,8},{36,12},{40,16},{44,20},{48,24},{52,28},{56,3... | collective-permute-start | bytes 73736 | tf_op jit(solution)/shard_map/ppermute | solution.py:336
  132.8 10.9 %copy-start.5 = (bf16[48,256]{1,0:T(8,128)(2,1)}, bf16[48,256]{1,0:T(8,128)(2,1)S(1)}, u32[]{:S(2)}) copy-start(bf16[48,256]{1,0:T(8,128)(2,1)S(1)} %collective-permute-done.9.refs_10_) | copy-start | bytes 73732
  132.8 10.3 %collective-permute-start.4 = (bf16[48,256]{1,0:T(8,128)(2,1)}, bf16[48,256]{1,0:T(8,128)(2,1)S(1)}, u32[]{:S(2)}, u32[]{:S(2)}) collective-permute-start(bf16[48,256]{1,0:T(8,128)(2,1)} %fold.1.refs_0_), channel_id=1, source_target_pairs={{20,0},{24,4},{28,8},{32,12},{36,16},{40,20},{44,24},{48,28},{52,3... | collective-permute-start | bytes 73736 | tf_op jit(solution)/shard_map/ppermute | solution.py:336
  133.8 9.9 %copy-start.6 = (bf16[48,256]{1,0:T(8,128)(2,1)}, bf16[48,256]{1,0:T(8,128)(2,1)S(1)}, u32[]{:S(2)}) copy-start(bf16[48,256]{1,0:T(8,128)(2,1)S(1)} %collective-permute-done.8.refs_9_) | copy-start | bytes 73732
  133.8 9.3 %collective-permute-start.3 = (bf16[48,256]{1,0:T(8,128)(2,1)}, bf16[48,256]{1,0:T(8,128)(2,1)S(1)}, u32[]{:S(2)}, u32[]{:S(2)}) collective-permute-start(bf16[48,256]{1,0:T(8,128)(2,1)} %fold.1.refs_0_), channel_id=1, source_target_pairs={{16,0},{20,4},{24,8},{28,12},{32,16},{36,20},{40,24},{44,28},{48,3... | collective-permute-start | bytes 73736 | tf_op jit(solution)/shard_map/ppermute | solution.py:336
  135.6 8.1 %copy-start.7 = (bf16[48,256]{1,0:T(8,128)(2,1)}, bf16[48,256]{1,0:T(8,128)(2,1)S(1)}, u32[]{:S(2)}) copy-start(bf16[48,256]{1,0:T(8,128)(2,1)S(1)} %collective-permute-done.7.refs_8_) | copy-start | bytes 73732
  135.6 7.6 %collective-permute-start.2 = (bf16[48,256]{1,0:T(8,128)(2,1)}, bf16[48,256]{1,0:T(8,128)(2,1)S(1)}, u32[]{:S(2)}, u32[]{:S(2)}) collective-permute-start(bf16[48,256]{1,0:T(8,128)(2,1)} %fold.1.refs_0_), channel_id=1, source_target_pairs={{12,0},{16,4},{20,8},{24,12},{28,16},{32,20},{36,24},{40,28},{44,3... | collective-permute-start | bytes 73736 | tf_op jit(solution)/shard_map/ppermute | solution.py:336
  138.1 5.6 %copy-start.8 = (bf16[48,256]{1,0:T(8,128)(2,1)}, bf16[48,256]{1,0:T(8,128)(2,1)S(1)}, u32[]{:S(2)}) copy-start(bf16[48,256]{1,0:T(8,128)(2,1)S(1)} %collective-permute-done.6.refs_7_) | copy-start | bytes 73732
  138.1 5.5 %collective-permute-start.1 = (bf16[48,256]{1,0:T(8,128)(2,1)}, bf16[48,256]{1,0:T(8,128)(2,1)S(1)}, u32[]{:S(2)}, u32[]{:S(2)}) collective-permute-start(bf16[48,256]{1,0:T(8,128)(2,1)} %fold.1.refs_0_), channel_id=1, source_target_pairs={{8,0},{12,4},{16,8},{20,12},{24,16},{28,20},{32,24},{36,28},{40,32... | collective-permute-start | bytes 73736 | tf_op jit(solution)/shard_map/ppermute | solution.py:336
  138.1 5.6 %copy-start.9 = (bf16[48,256]{1,0:T(8,128)(2,1)}, bf16[48,256]{1,0:T(8,128)(2,1)S(1)}, u32[]{:S(2)}) copy-start(bf16[48,256]{1,0:T(8,128)(2,1)S(1)} %collective-permute-done.5.refs_6_) | copy-start | bytes 73732
  138.2 5.5 %collective-permute-start = (bf16[48,256]{1,0:T(8,128)(2,1)}, bf16[48,256]{1,0:T(8,128)(2,1)S(1)}, u32[]{:S(2)}, u32[]{:S(2)}) collective-permute-start(bf16[48,256]{1,0:T(8,128)(2,1)} %fold.1.refs_0_), channel_id=1, source_target_pairs={{4,0},{8,4},{12,8},{16,12},{20,16},{24,20},{28,24},{32,28},{36,32}... | collective-permute-start | bytes 73736 | tf_op jit(solution)/shard_map/ppermute | solution.py:336
  143.1 0.6 copy-start.10
  143.2 0.6 copy-start.11
  143.2 0.6 copy-start.12
  143.7 0.6 copy-start.13
  143.7 0.6 copy-start.14
  176.2 3.9 %collective-permute-start.15 = (bf16[32,112,256]{2,1,0:T(8,128)(2,1)S(1)}, bf16[32,112,256]{2,1,0:T(8,128)(2,1)S(1)}, u32[]{:S(2)}, u32[]{:S(2)}) collective-permute-start(bf16[32,112,256]{2,1,0:T(8,128)(2,1)S(1)} %get-tuple-element.15), channel_id=1, source_target_pairs={{0,1},{1,0},{2,3},{3,2},{4,5},{5,4},{6,7},{7,6},{8,9},{9,8},{10,11... | collective-permute-start | bytes 5505032 | tf_op jit(solution)/shard_map/ppermute | solution.py:353
  218.0 4.3 %collective-permute-start.16 = (bf16[112,256]{1,0:T(8,128)(2,1)S(1)}, bf16[112,256]{1,0:T(8,128)(2,1)S(1)}, u32[]{:S(2)}, u32[]{:S(2)}) collective-permute-start(bf16[112,256]{1,0:T(8,128)(2,1)S(1)} %reduce_sum.12.own), channel_id=1, source_target_pairs={{0,64},{64,0},{1,65},{65,1},{2,66},{66,2},{3,67},{67,3},{4,68},{68... | collective-permute-start | bytes 172040 | tf_op jit(solution)/shard_map/ppermute | solution.py:357

commit v6 on v5

--- a/solution.py
+++ b/solution.py
@@ -23,10 +23,11 @@
     height, width, depth = held.shape
     rest = width - LANES
     devices = depth // q_own
-    spans = [(at, min(WIN, height - at)) for at in range(0, height, WIN)]
+    parts = [(pl.ds(at, WIN), pl.ds(0, LANES)) for at in range(0, FULL, WIN)]
+    parts += [(pl.ds(0, height), pl.ds(LANES, rest)), (pl.ds(FULL, height - FULL), pl.ds(0, LANES))]
     copies = [
-        pltpu.make_async_copy(source.at[at : at + n], held.at[at : at + n], sem.at[k])
-        for k, (at, n) in enumerate(spans)
+        pltpu.make_async_copy(source.at[part], held.at[part], sem.at[k])
+        for k, part in enumerate(parts)
     ]
     for copy in copies:
         copy.start()
@@ -70,7 +71,7 @@
 
 
 def pack_call(own, q_own, source):
-    height, _, depth = source.shape
+    _, _, depth = source.shape
     source = pltpu.with_memory_space_constraint(source, pltpu.HBM)
     return pl.pallas_call(
         functools.partial(pack, own, q_own),
@@ -80,7 +81,7 @@
         scratch_shapes=[
             pltpu.VMEM(source.shape, jnp.bfloat16),
             pltpu.VMEM((LONG // WIN, depth // q_own, WIN, LANES), jnp.bfloat16),
-            pltpu.SemaphoreType.DMA((-(-height // WIN),)),
+            pltpu.SemaphoreType.DMA((FULL // WIN + 2,)),
             pltpu.SemaphoreType.DMA((LONG // WIN,)),
         ],
         compiler_params=pltpu.CompilerParams(vmem_limit_bytes=20 * 2**20),

time: 224 us -> 223 us (level)
  no operation moved by 1% of the time
where the time goes in v6:
time: 223 us
  waiting for transfers between devices  81.5 us (37%)
  starting transfers between devices  50.3 us (23%)
  Pallas kernels  44.1 us (20%)
  blocking collectives  37.2 us (17%)
  local copies, waits for them, and re-layouts  5.63 us (3%)
  other arithmetic  3.07 us (1%)
    all_to_all x2, waiting for transfers between devices, swap(): return lax.all_to_all(array, axis, split_axis=0, concat_axis=0, tiled=True)  39 us
    all_to_all x1, blocking collectives, swap(): return lax.all_to_all(array, axis, split_axis=0, concat_axis=0, tiled=True)  37.2 us
    ppermute x15, waiting for transfers between devices, all_of(): found.append(lax.ppermute(folded, axis, pairs))  35.6 us
    ppermute x15, starting transfers between devices, all_of(): found.append(lax.ppermute(folded, axis, pairs))  29.6 us
    pallas_call x2, Pallas kernels, dress_call(): pl.pallas_call(functools.partial(dress, own, last), out_shape=out_shape,...  24.7 us
    all_to_all x2, starting transfers between devices, swap(): return lax.all_to_all(array, axis, split_axis=0, concat_axis=0, tiled=True)  19.5 us
    pallas_call x2, Pallas kernels, pack_call(): pl.pallas_call(functools.partial(pack, own, q_own), out_shape=pltpu.HBM((...  15.2 us
  transfers between devices with their start and end apart: 19, of which 6 were waited for; matrix products, arithmetic and copies ran while one was open for 3% of the time, Pallas kernels for 10%

profile of v6, /device:TPU:0, one launch (start us, length us, event | category | flops | bytes accessed | tf_op | source)
XLA Modules:
  0.0 222.8 jit_solution(14694463736506788945)
XLA Ops:
  0.6 7.6 %pack.3 = bf16[64,112,256]{2,1,0:T(8,128)(2,1)} custom-call(bf16[84,336,128]{2,1,0:T(8,128)(2,1)} %bitcast.17), custom_call_target="tpu_custom_call" | custom-call | flops 5000000000 | bytes 10000000 | tf_op jit(solution)/shard_map/pack/pallas_call | solution.py:76
  8.2 11.6 %all-to-all-start.1 = ((bf16[64,112,256]{2,1,0:T(8,128)(2,1)}), bf16[64,112,256]{2,1,0:T(8,128)(2,1)}, u32[]{:S(2)}, u32[]{:S(2)}) async-start(bf16[64,112,256]{2,1,0:T(8,128)(2,1)} %pack.3), calls=%async_computation.1 | async-start | bytes 7340032 | tf_op jit(solution)/shard_map/all_to_all | solution.py:327
  19.8 7.6 %pack.2 = bf16[64,112,256]{2,1,0:T(8,128)(2,1)} custom-call(bf16[84,336,128]{2,1,0:T(8,128)(2,1)} %bitcast.18), custom_call_target="tpu_custom_call" | custom-call | flops 5000000000 | bytes 10000000 | tf_op jit(solution)/shard_map/pack/pallas_call | solution.py:76
  27.5 39.0 %all-to-all-done.1.pieces = bf16[64,112,256]{2,1,0:T(8,128)(2,1)} async-done(((bf16[64,112,256]{2,1,0:T(8,128)(2,1)}), bf16[64,112,256]{2,1,0:T(8,128)(2,1)}, u32[]{:S(2)}, u32[]{:S(2)}) %all-to-all-start.1) | async-done | bytes 3670048 | tf_op jit(solution)/shard_map/all_to_all | solution.py:327
  66.5 7.9 %all-to-all-start = ((bf16[64,112,256]{2,1,0:T(8,128)(2,1)}), bf16[64,112,256]{2,1,0:T(8,128)(2,1)}, u32[]{:S(2)}, u32[]{:S(2)}) async-start(bf16[64,112,256]{2,1,0:T(8,128)(2,1)} %pack.2), calls=%async_computation | async-start | bytes 7340032 | tf_op jit(solution)/shard_map/all_to_all | solution.py:327
  74.4 1.5 fold.1.refs_0_
  75.9 1.5 collective-permute-start.14
  77.4 2.7 %collective-permute-start.13 = (bf16[48,256]{1,0:T(8,128)(2,1)}, bf16[48,256]{1,0:T(8,128)(2,1)S(1)}, u32[]{:S(2)}, u32[]{:S(2)}) collective-permute-start(bf16[48,256]{1,0:T(8,128)(2,1)} %fold.1.refs_0_), channel_id=1, source_target_pairs={{56,0},{60,4},{0,8},{4,12},{8,16},{12,20},{16,24},{20,28},{24,32},... | collective-permute-start | bytes 73736 | tf_op jit(solution)/shard_map/ppermute | solution.py:337
  80.0 2.4 %collective-permute-start.12 = (bf16[48,256]{1,0:T(8,128)(2,1)}, bf16[48,256]{1,0:T(8,128)(2,1)S(1)}, u32[]{:S(2)}, u32[]{:S(2)}) collective-permute-start(bf16[48,256]{1,0:T(8,128)(2,1)} %fold.1.refs_0_), channel_id=1, source_target_pairs={{52,0},{56,4},{60,8},{0,12},{4,16},{8,20},{12,24},{16,28},{20,32},... | collective-permute-start | bytes 73736 | tf_op jit(solution)/shard_map/ppermute | solution.py:337
  82.4 1.6 collective-permute-start.11
  84.0 1.3 collective-permute-start.10
  85.4 35.0 %collective-permute-done.14.refs_15_ = bf16[48,256]{1,0:T(8,128)(2,1)S(1)} collective-permute-done((bf16[48,256]{1,0:T(8,128)(2,1)}, bf16[48,256]{1,0:T(8,128)(2,1)S(1)}, u32[]{:S(2)}, u32[]{:S(2)}) %collective-permute-start.14) | collective-permute-done | bytes 24608 | tf_op jit(solution)/shard_map/ppermute | solution.py:337
  120.3 0.2 collective-permute-start.9
  120.6 0.1 collective-permute-done.13.refs_14_
  120.7 1.8 collective-permute-start.8
  122.5 3.6 %collective-permute-start.7 = (bf16[48,256]{1,0:T(8,128)(2,1)}, bf16[48,256]{1,0:T(8,128)(2,1)S(1)}, u32[]{:S(2)}, u32[]{:S(2)}) collective-permute-start(bf16[48,256]{1,0:T(8,128)(2,1)} %fold.1.refs_0_), channel_id=1, source_target_pairs={{32,0},{36,4},{40,8},{44,12},{48,16},{52,20},{56,24},{60,28},{0,32... | collective-permute-start | bytes 73736 | tf_op jit(solution)/shard_map/ppermute | solution.py:337
  126.0 0.0 collective-permute-done.11.refs_12_
  126.0 1.1 collective-permute-start.6
  127.1 5.6 %collective-permute-start.5 = (bf16[48,256]{1,0:T(8,128)(2,1)}, bf16[48,256]{1,0:T(8,128)(2,1)S(1)}, u32[]{:S(2)}, u32[]{:S(2)}) collective-permute-start(bf16[48,256]{1,0:T(8,128)(2,1)} %fold.1.refs_0_), channel_id=1, source_target_pairs={{24,0},{28,4},{32,8},{36,12},{40,16},{44,20},{48,24},{52,28},{56,3... | collective-permute-start | bytes 73736 | tf_op jit(solution)/shard_map/ppermute | solution.py:337
  132.7 0.0 collective-permute-done.9.refs_10_
  132.7 0.8 collective-permute-start.4
  133.5 1.8 collective-permute-start.3
  135.3 2.5 %collective-permute-start.2 = (bf16[48,256]{1,0:T(8,128)(2,1)}, bf16[48,256]{1,0:T(8,128)(2,1)S(1)}, u32[]{:S(2)}, u32[]{:S(2)}) collective-permute-start(bf16[48,256]{1,0:T(8,128)(2,1)} %fold.1.refs_0_), channel_id=1, source_target_pairs={{12,0},{16,4},{20,8},{24,12},{28,16},{32,20},{36,24},{40,28},{44,3... | collective-permute-start | bytes 73736 | tf_op jit(solution)/shard_map/ppermute | solution.py:337
  137.8 0.0 collective-permute-done.6.refs_7_
  137.9 2.7 %collective-permute-start = (bf16[48,256]{1,0:T(8,128)(2,1)}, bf16[48,256]{1,0:T(8,128)(2,1)S(1)}, u32[]{:S(2)}, u32[]{:S(2)}) collective-permute-start(bf16[48,256]{1,0:T(8,128)(2,1)} %fold.1.refs_0_), channel_id=1, source_target_pairs={{4,0},{8,4},{12,8},{16,12},{20,16},{24,20},{28,24},{32,28},{36,32}... | collective-permute-start | bytes 73736 | tf_op jit(solution)/shard_map/ppermute | solution.py:337
  140.6 2.2 fusion.14.sel
  142.9 0.5 collective-permute-done.1.refs_2_
  143.5 0.5 copy-done.13
  144.0 0.0 copy-done.14
  144.0 2.0 join.1
  146.0 1.2 copy.6
  147.3 0.3 pad.12
  147.5 0.9 copy.7
  148.4 0.1 pad.13
  148.5 1.0 reshape.29
  149.5 1.2 pad.14
  150.6 0.3 copy.12.cols
  150.9 0.3 copy.11.win
  151.2 11.5 %dress_first.1 = (bf16[2,1344,1344]{2,1,0:T(8,128)(2,1)}, bf16[4,384,1536]{2,1,0:T(8,128)(2,1)}) custom-call(bf16[64,112,256]{2,1,0:T(8,128)(2,1)} %all-to-all-done.1.pieces, bf16[256,1536]{1,0:T(8,128)(2,1)S(1)} %copy.11.win, bf16[256,1536]{1,0:T(8,128)(2,1)S(1)} %copy.12.cols, bf16[1536,256]{1,0:T(8,128)(2,1)S(1)} %fusion.14.sel), custom_call_target="tpu_custom_call" | custom-call | flops 10000000000 | bytes 10000000 | tf_op jit(solution)/shard_map/dress_first/pallas_call | solution.py:222
  162.7 13.2 %dress_last.1 = (bf16[2,1344,1344]{2,1,0:T(8,128)(2,1)}, bf16[32,112,256]{2,1,0:T(8,128)(2,1)S(1)}, bf16[32,112,256]{2,1,0:T(8,128)(2,1)S(1)}) custom-call(bf16[64,112,256]{2,1,0:T(8,128)(2,1)} %all-to-all-done.pieces, bf16[256,1536]{1,0:T(8,128)(2,1)S(1)} %copy.11.win, bf16[256,1536]{1,0:T(8,128)(2,1)S(1)} %copy.12.cols, ...), custom_call_target="tpu_custom_call", output_to_operand_aliasing={{0}: (6, {})} | custom-call | flops 10000000000 | bytes 10000000 | tf_op jit(solution)/shard_map/dress_last/pallas_call | solution.py:222
  175.9 0.1 collective-permute-start.15
  176.0 3.8 %collective-permute-done.15 = bf16[32,112,256]{2,1,0:T(8,128)(2,1)S(1)} collective-permute-done((bf16[32,112,256]{2,1,0:T(8,128)(2,1)S(1)}, bf16[32,112,256]{2,1,0:T(8,128)(2,1)S(1)}, u32[]{:S(2)}, u32[]{:S(2)}) %collective-permute-start.15) | collective-permute-done | bytes 1835040 | tf_op jit(solution)/shard_map/ppermute | solution.py:354
  179.8 0.5 add_convert_fusion
  180.3 37.2 %all_to_all.15 = bf16[32,112,256]{2,1,0:T(8,128)(2,1)S(1)} all-to-all(bf16[32,112,256]{2,1,0:T(8,128)(2,1)S(1)} %add_convert_fusion), channel_id=1, replica_groups=mesh['pb'=2,'row_0'=4,'row_1'=4,'col_0'=2,'col_1'=2] {'row_0','row_1','c..., dimensions={0} | all-to-all | bytes 3670016 | tf_op jit(solution)/shard_map/all_to_all | solution.py:327
  217.5 0.3 reduce_sum.12.own
  217.8 1.1 collective-permute-start.16
  218.8 3.2 %collective-permute-done.16.other = bf16[112,256]{1,0:T(8,128)(2,1)S(1)} collective-permute-done((bf16[112,256]{1,0:T(8,128)(2,1)S(1)}, bf16[112,256]{1,0:T(8,128)(2,1)S(1)}, u32[]{:S(2)}, u32[]{:S(2)}) %collective-permute-start.16) | collective-permute-done | bytes 57376 | tf_op jit(solution)/shard_map/ppermute | solution.py:358
  222.0 0.7 finish.1
  (45 shorter events, 0.1 us)
Async XLA Ops:
  8.2 58.3 %all-to-all-start.1 = ((bf16[64,112,256]{2,1,0:T(8,128)(2,1)}), bf16[64,112,256]{2,1,0:T(8,128)(2,1)}, u32[]{:S(2)}, u32[]{:S(2)}) async-start(bf16[64,112,256]{2,1,0:T(8,128)(2,1)} %pack.3), calls=%async_computation.1 | async-start | bytes 7340032 | tf_op jit(solution)/shard_map/all_to_all | solution.py:327
  66.5 96.3 %all-to-all-start = ((bf16[64,112,256]{2,1,0:T(8,128)(2,1)}), bf16[64,112,256]{2,1,0:T(8,128)(2,1)}, u32[]{:S(2)}, u32[]{:S(2)}) async-start(bf16[64,112,256]{2,1,0:T(8,128)(2,1)} %pack.2), calls=%async_computation | async-start | bytes 7340032 | tf_op jit(solution)/shard_map/all_to_all | solution.py:327
  75.9 44.5 %collective-permute-start.14 = (bf16[48,256]{1,0:T(8,128)(2,1)}, bf16[48,256]{1,0:T(8,128)(2,1)S(1)}, u32[]{:S(2)}, u32[]{:S(2)}) collective-permute-start(bf16[48,256]{1,0:T(8,128)(2,1)} %fold.1.refs_0_), channel_id=1, source_target_pairs={{60,0},{0,4},{4,8},{8,12},{12,16},{16,20},{20,24},{24,28},{28,32},... | collective-permute-start | bytes 73736 | tf_op jit(solution)/shard_map/ppermute | solution.py:337
  77.4 43.3 %collective-permute-start.13 = (bf16[48,256]{1,0:T(8,128)(2,1)}, bf16[48,256]{1,0:T(8,128)(2,1)S(1)}, u32[]{:S(2)}, u32[]{:S(2)}) collective-permute-start(bf16[48,256]{1,0:T(8,128)(2,1)} %fold.1.refs_0_), channel_id=1, source_target_pairs={{56,0},{60,4},{0,8},{4,12},{8,16},{12,20},{16,24},{20,28},{24,32},... | collective-permute-start | bytes 73736 | tf_op jit(solution)/shard_map/ppermute | solution.py:337
  80.0 42.4 %collective-permute-start.12 = (bf16[48,256]{1,0:T(8,128)(2,1)}, bf16[48,256]{1,0:T(8,128)(2,1)S(1)}, u32[]{:S(2)}, u32[]{:S(2)}) collective-permute-start(bf16[48,256]{1,0:T(8,128)(2,1)} %fold.1.refs_0_), channel_id=1, source_target_pairs={{52,0},{56,4},{60,8},{0,12},{4,16},{8,20},{12,24},{16,28},{20,32},... | collective-permute-start | bytes 73736 | tf_op jit(solution)/shard_map/ppermute | solution.py:337
  82.4 43.6 %collective-permute-start.11 = (bf16[48,256]{1,0:T(8,128)(2,1)}, bf16[48,256]{1,0:T(8,128)(2,1)S(1)}, u32[]{:S(2)}, u32[]{:S(2)}) collective-permute-start(bf16[48,256]{1,0:T(8,128)(2,1)} %fold.1.refs_0_), channel_id=1, source_target_pairs={{48,0},{52,4},{56,8},{60,12},{0,16},{4,20},{8,24},{12,28},{16,32},... | collective-permute-start | bytes 73736 | tf_op jit(solution)/shard_map/ppermute | solution.py:337
  84.0 43.1 %collective-permute-start.10 = (bf16[48,256]{1,0:T(8,128)(2,1)}, bf16[48,256]{1,0:T(8,128)(2,1)S(1)}, u32[]{:S(2)}, u32[]{:S(2)}) collective-permute-start(bf16[48,256]{1,0:T(8,128)(2,1)} %fold.1.refs_0_), channel_id=1, source_target_pairs={{44,0},{48,4},{52,8},{56,12},{60,16},{0,20},{4,24},{8,28},{12,32},... | collective-permute-start | bytes 73736 | tf_op jit(solution)/shard_map/ppermute | solution.py:337
  120.3 23.1 %copy-start = (bf16[48,256]{1,0:T(8,128)(2,1)}, bf16[48,256]{1,0:T(8,128)(2,1)S(1)}, u32[]{:S(2)}) copy-start(bf16[48,256]{1,0:T(8,128)(2,1)S(1)} %collective-permute-done.14.refs_15_) | copy-start | bytes 73732
  120.3 12.4 %collective-permute-start.9 = (bf16[48,256]{1,0:T(8,128)(2,1)}, bf16[48,256]{1,0:T(8,128)(2,1)S(1)}, u32[]{:S(2)}, u32[]{:S(2)}) collective-permute-start(bf16[48,256]{1,0:T(8,128)(2,1)} %fold.1.refs_0_), channel_id=1, source_target_pairs={{40,0},{44,4},{48,8},{52,12},{56,16},{60,20},{0,24},{4,28},{8,32},... | collective-permute-start | bytes 73736 | tf_op jit(solution)/shard_map/ppermute | solution.py:337
  120.7 22.7 %copy-start.1 = (bf16[48,256]{1,0:T(8,128)(2,1)}, bf16[48,256]{1,0:T(8,128)(2,1)S(1)}, u32[]{:S(2)}) copy-start(bf16[48,256]{1,0:T(8,128)(2,1)S(1)} %collective-permute-done.13.refs_14_) | copy-start | bytes 73732
  120.7 12.9 %collective-permute-start.8 = (bf16[48,256]{1,0:T(8,128)(2,1)}, bf16[48,256]{1,0:T(8,128)(2,1)S(1)}, u32[]{:S(2)}, u32[]{:S(2)}) collective-permute-start(bf16[48,256]{1,0:T(8,128)(2,1)} %fold.1.refs_0_), channel_id=1, source_target_pairs={{36,0},{40,4},{44,8},{48,12},{52,16},{56,20},{60,24},{0,28},{4,32}... | collective-permute-start | bytes 73736 | tf_op jit(solution)/shard_map/ppermute | solution.py:337
  122.5 21.0 %copy-start.2 = (bf16[48,256]{1,0:T(8,128)(2,1)}, bf16[48,256]{1,0:T(8,128)(2,1)S(1)}, u32[]{:S(2)}) copy-start(bf16[48,256]{1,0:T(8,128)(2,1)S(1)} %collective-permute-done.12.refs_13_) | copy-start | bytes 73732
  122.5 12.9 %collective-permute-start.7 = (bf16[48,256]{1,0:T(8,128)(2,1)}, bf16[48,256]{1,0:T(8,128)(2,1)S(1)}, u32[]{:S(2)}, u32[]{:S(2)}) collective-permute-start(bf16[48,256]{1,0:T(8,128)(2,1)} %fold.1.refs_0_), channel_id=1, source_target_pairs={{32,0},{36,4},{40,8},{44,12},{48,16},{52,20},{56,24},{60,28},{0,32... | collective-permute-start | bytes 73736 | tf_op jit(solution)/shard_map/ppermute | solution.py:337
  126.0 17.4 %copy-start.3 = (bf16[48,256]{1,0:T(8,128)(2,1)}, bf16[48,256]{1,0:T(8,128)(2,1)S(1)}, u32[]{:S(2)}) copy-start(bf16[48,256]{1,0:T(8,128)(2,1)S(1)} %collective-permute-done.11.refs_12_) | copy-start | bytes 73732
  126.0 11.8 %collective-permute-start.6 = (bf16[48,256]{1,0:T(8,128)(2,1)}, bf16[48,256]{1,0:T(8,128)(2,1)S(1)}, u32[]{:S(2)}, u32[]{:S(2)}) collective-permute-start(bf16[48,256]{1,0:T(8,128)(2,1)} %fold.1.refs_0_), channel_id=1, source_target_pairs={{28,0},{32,4},{36,8},{40,12},{44,16},{48,20},{52,24},{56,28},{60,3... | collective-permute-start | bytes 73736 | tf_op jit(solution)/shard_map/ppermute | solution.py:337
  127.1 16.3 %copy-start.4 = (bf16[48,256]{1,0:T(8,128)(2,1)}, bf16[48,256]{1,0:T(8,128)(2,1)S(1)}, u32[]{:S(2)}) copy-start(bf16[48,256]{1,0:T(8,128)(2,1)S(1)} %collective-permute-done.10.refs_11_) | copy-start | bytes 73732
  127.1 10.7 %collective-permute-start.5 = (bf16[48,256]{1,0:T(8,128)(2,1)}, bf16[48,256]{1,0:T(8,128)(2,1)S(1)}, u32[]{:S(2)}, u32[]{:S(2)}) collective-permute-start(bf16[48,256]{1,0:T(8,128)(2,1)} %fold.1.refs_0_), channel_id=1, source_target_pairs={{24,0},{28,4},{32,8},{36,12},{40,16},{44,20},{48,24},{52,28},{56,3... | collective-permute-start | bytes 73736 | tf_op jit(solution)/shard_map/ppermute | solution.py:337
  132.7 10.7 %copy-start.5 = (bf16[48,256]{1,0:T(8,128)(2,1)}, bf16[48,256]{1,0:T(8,128)(2,1)S(1)}, u32[]{:S(2)}) copy-start(bf16[48,256]{1,0:T(8,128)(2,1)S(1)} %collective-permute-done.9.refs_10_) | copy-start | bytes 73732
  132.7 10.1 %collective-permute-start.4 = (bf16[48,256]{1,0:T(8,128)(2,1)}, bf16[48,256]{1,0:T(8,128)(2,1)S(1)}, u32[]{:S(2)}, u32[]{:S(2)}) collective-permute-start(bf16[48,256]{1,0:T(8,128)(2,1)} %fold.1.refs_0_), channel_id=1, source_target_pairs={{20,0},{24,4},{28,8},{32,12},{36,16},{40,20},{44,24},{48,28},{52,3... | collective-permute-start | bytes 73736 | tf_op jit(solution)/shard_map/ppermute | solution.py:337
  133.5 9.9 %copy-start.6 = (bf16[48,256]{1,0:T(8,128)(2,1)}, bf16[48,256]{1,0:T(8,128)(2,1)S(1)}, u32[]{:S(2)}) copy-start(bf16[48,256]{1,0:T(8,128)(2,1)S(1)} %collective-permute-done.8.refs_9_) | copy-start | bytes 73732
  133.5 9.3 %collective-permute-start.3 = (bf16[48,256]{1,0:T(8,128)(2,1)}, bf16[48,256]{1,0:T(8,128)(2,1)S(1)}, u32[]{:S(2)}, u32[]{:S(2)}) collective-permute-start(bf16[48,256]{1,0:T(8,128)(2,1)} %fold.1.refs_0_), channel_id=1, source_target_pairs={{16,0},{20,4},{24,8},{28,12},{32,16},{36,20},{40,24},{44,28},{48,3... | collective-permute-start | bytes 73736 | tf_op jit(solution)/shard_map/ppermute | solution.py:337
  135.3 8.1 %copy-start.7 = (bf16[48,256]{1,0:T(8,128)(2,1)}, bf16[48,256]{1,0:T(8,128)(2,1)S(1)}, u32[]{:S(2)}) copy-start(bf16[48,256]{1,0:T(8,128)(2,1)S(1)} %collective-permute-done.7.refs_8_) | copy-start | bytes 73732
  135.3 7.6 %collective-permute-start.2 = (bf16[48,256]{1,0:T(8,128)(2,1)}, bf16[48,256]{1,0:T(8,128)(2,1)S(1)}, u32[]{:S(2)}, u32[]{:S(2)}) collective-permute-start(bf16[48,256]{1,0:T(8,128)(2,1)} %fold.1.refs_0_), channel_id=1, source_target_pairs={{12,0},{16,4},{20,8},{24,12},{28,16},{32,20},{36,24},{40,28},{44,3... | collective-permute-start | bytes 73736 | tf_op jit(solution)/shard_map/ppermute | solution.py:337
  137.8 5.6 %copy-start.8 = (bf16[48,256]{1,0:T(8,128)(2,1)}, bf16[48,256]{1,0:T(8,128)(2,1)S(1)}, u32[]{:S(2)}) copy-start(bf16[48,256]{1,0:T(8,128)(2,1)S(1)} %collective-permute-done.6.refs_7_) | copy-start | bytes 73732
  137.8 5.5 %collective-permute-start.1 = (bf16[48,256]{1,0:T(8,128)(2,1)}, bf16[48,256]{1,0:T(8,128)(2,1)S(1)}, u32[]{:S(2)}, u32[]{:S(2)}) collective-permute-start(bf16[48,256]{1,0:T(8,128)(2,1)} %fold.1.refs_0_), channel_id=1, source_target_pairs={{8,0},{12,4},{16,8},{20,12},{24,16},{28,20},{32,24},{36,28},{40,32... | collective-permute-start | bytes 73736 | tf_op jit(solution)/shard_map/ppermute | solution.py:337
  137.9 5.6 %copy-start.9 = (bf16[48,256]{1,0:T(8,128)(2,1)}, bf16[48,256]{1,0:T(8,128)(2,1)S(1)}, u32[]{:S(2)}) copy-start(bf16[48,256]{1,0:T(8,128)(2,1)S(1)} %collective-permute-done.5.refs_6_) | copy-start | bytes 73732
  137.9 5.5 %collective-permute-start = (bf16[48,256]{1,0:T(8,128)(2,1)}, bf16[48,256]{1,0:T(8,128)(2,1)S(1)}, u32[]{:S(2)}, u32[]{:S(2)}) collective-permute-start(bf16[48,256]{1,0:T(8,128)(2,1)} %fold.1.refs_0_), channel_id=1, source_target_pairs={{4,0},{8,4},{12,8},{16,12},{20,16},{24,20},{28,24},{32,28},{36,32}... | collective-permute-start | bytes 73736 | tf_op jit(solution)/shard_map/ppermute | solution.py:337
  142.9 0.6 copy-start.10
  142.9 0.6 copy-start.11
  142.9 0.6 copy-start.12
  143.4 0.6 copy-start.13
  143.4 0.6 copy-start.14
  175.9 3.9 %collective-permute-start.15 = (bf16[32,112,256]{2,1,0:T(8,128)(2,1)S(1)}, bf16[32,112,256]{2,1,0:T(8,128)(2,1)S(1)}, u32[]{:S(2)}, u32[]{:S(2)}) collective-permute-start(bf16[32,112,256]{2,1,0:T(8,128)(2,1)S(1)} %get-tuple-element.15), channel_id=1, source_target_pairs={{0,1},{1,0},{2,3},{3,2},{4,5},{5,4},{6,7},{7,6},{8,9},{9,8},{10,11... | collective-permute-start | bytes 5505032 | tf_op jit(solution)/shard_map/ppermute | solution.py:354
  217.8 4.3 %collective-permute-start.16 = (bf16[112,256]{1,0:T(8,128)(2,1)S(1)}, bf16[112,256]{1,0:T(8,128)(2,1)S(1)}, u32[]{:S(2)}, u32[]{:S(2)}) collective-permute-start(bf16[112,256]{1,0:T(8,128)(2,1)S(1)} %reduce_sum.12.own), channel_id=1, source_target_pairs={{0,64},{64,0},{1,65},{65,1},{2,66},{66,2},{3,67},{67,3},{4,68},{68... | collective-permute-start | bytes 172040 | tf_op jit(solution)/shard_map/ppermute | solution.py:358
